TPU v7x, 32 devices: a whole 2x2x4 slice. The times are simulated.
32 devices in a mesh: gx: 4 (over z), gy: 2 (over y), gz: 4 (over x, core).
Axes of the slice: x: 2, y: 2, z: 4, core: 2. Of those that a mesh axis runs over, the one named last changes fastest.
Arguments:
- blocks: bfloat16 [8, 2, 8, 27, 128, 128], P('gx', 'gy', 'gz')
- pattern: int32 [8, 2, 8, 27], P('gx', 'gy'), may hold values 0 or 1
- order: int32 [8, 2, 8], P('gx', 'gy'), may hold values from 0 to 7, each once within a row
- start: float32 [8, 2, 8, 128], P('gx', 'gy', 'gz'), may hold values from -6 to 6
- rhs: float32 [8, 2, 8, 128], P('gx', 'gy', 'gz'), may hold values from -6 to 6
Outputs:
- smoothed: float32 [8, 2, 8, 128], P('gx', 'gy', 'gz')
- remainder: float32 [8, 2, 8, 128], P('gx', 'gy', 'gz')
Inputs may be any that keep to these rules, and one draw needn't show every extreme that they name: `order`: in every grid column the 8 slots name each plane exactly once. `pattern`: entry 13 is ignored.
All inputs are finite; a program needn't handle non-finite values. No bound on the sum of `pattern` on one device may be relied on, other than what follows from the above.
Results may differ from a plain program's by a relative error of at most 0.0081.
Values may be sent and summed in bfloat16 or wider, within the bound.
No kernel may reach another device: no remote copies, remote signals or barrier semaphores. Data moves between devices by JAX's collectives and lax.ppermute only.
A program may use at most 64 MiB of HBM per device.

v0:
```python
import jax
import jax.numpy as jnp
from jax import lax
from jax.sharding import PartitionSpec as P

DEG = 4


def padded_2(cells, sides, width):
    for axis, dim in sides:
        count = lax.axis_size(axis)
        ends = count - 1
        head = lax.slice_in_dim(cells, 0, width, axis=dim)
        tail = lax.slice_in_dim(cells, cells.shape[dim] - width, cells.shape[dim], axis=dim)
        cells = jnp.concatenate(
            [
                lax.ppermute(tail, axis, [(i, (i + 1) % count) for i in range(ends)]),
                cells,
                lax.ppermute(head, axis, [((i + 1) % count, i) for i in range(ends)]),
            ],
            axis=dim,
        )
    return cells


def coupled_product(matrix, planes, rows, present):
    padded = padded_2(planes, (("gx", 0), ("gy", 1)), 1)
    padded = jnp.pad(padded, ((0, 0), (0, 0), (1, 1), (0, 0)))
    span_x, span_y = (planes.shape[0], planes.shape[1])
    height = padded.shape[2]
    keeping = jnp.where(jnp.arange(27) == 13, 1, present).astype(jnp.float32)
    offsets = jnp.arange(3, dtype=jnp.int32)
    places = jnp.arange(height, dtype=jnp.int32)
    target = rows[..., None, None] + offsets[:, None]
    select = (target == places).astype(jnp.float32)
    pieces = []
    for step_a in range(3):
        for step_b in range(3):
            column = padded[step_a : step_a + span_x, step_b : step_b + span_y]
            first = 9 * step_a + 3 * step_b
            table = (select * keeping[..., first : first + 3, None]).astype(jnp.bfloat16)
            picked = jnp.einsum(
                "xyscp,xypw->xyscw", table, column, preferred_element_type=jnp.float32
            )
            pieces.append(picked.astype(jnp.bfloat16))
    gathered = jnp.stack(pieces, axis=3)
    gathered = gathered.reshape(gathered.shape[:3] + (27, gathered.shape[-1]))
    return jnp.einsum("xysoj,xysoij->xysi", gathered, matrix, preferred_element_type=jnp.float32)


def by_plane(vector, order):
    places = jnp.arange(order.shape[2], dtype=jnp.int32)
    table = (order[..., None] == places).astype(jnp.bfloat16)
    moved = jnp.einsum("xysp,xysw->xypw", table, vector, preferred_element_type=jnp.float32)
    return moved.astype(jnp.bfloat16)


def local(blocks, pattern, order, start, rhs):
    depth = blocks.shape[2]
    first = lax.axis_index("gz") * depth
    smoothed, target = (start, rhs)
    rows = lax.dynamic_slice_in_dim(order, first, depth, 2)
    present = lax.dynamic_slice_in_dim(pattern, first, depth, 2)

    def operator(vector):
        column = lax.all_gather(vector.astype(jnp.bfloat16), "gz", axis=2, tiled=True)
        planes = by_plane(column, order)
        return coupled_product(blocks, planes, rows, present)

    center = 1.0
    spread = 0.8
    sigma = center / spread
    rho = 1.0 / sigma
    remainder = target - operator(smoothed)
    search = remainder / center
    for number in range(DEG):
        smoothed = smoothed + search
        remainder = remainder - operator(search)
        if number + 1 < DEG:
            following = 1.0 / (2.0 * sigma - rho)
            search = following * rho * search + 2.0 * following / spread * remainder
            rho = following
    return (smoothed, remainder)


def solution(mesh):
    in_specs = (
        P("gx", "gy", "gz", None, None, None),
        P("gx", "gy", None, None),
        P("gx", "gy", None),
        P("gx", "gy", "gz", None),
        P("gx", "gy", "gz", None),
    )
    out_specs = (P("gx", "gy", "gz", None), P("gx", "gy", "gz", None))
    return jax.shard_map(local, mesh=mesh, in_specs=in_specs, out_specs=out_specs, check_vma=False)
```

profile of v0, /device:TPU:0, one launch (start us, length us, event | category | flops | bytes accessed | tf_op | source)
XLA Modules:
  0.0 124.0 jit_solution(8607130431343149875)
XLA Ops:
  0.7 0.8 copy.155
  1.5 6.1 %all_gather.15 = bf16[2,1,8,128]{3,0,1,2:T(2,128)(2,1)S(1)} all-gather(bf16[2,1,2,128]{3,0,1,2:T(2,128)(2,1)S(1)} %copy.155), channel_id=1, replica_groups=mesh['gx'=4,'gy'=2,'gz'=4] {'gz'}, dimensions={2}, use_global_device_ids=true | all-gather | bytes 5120 | tf_op jit(solution)/shard_map/all_gather | solution.py:66
  7.6 0.8 convolution_convert_fusion.49
  8.4 0.6 slice_bitcast_fusion.107
  9.0 4.0 %collective-permute-start = (bf16[1,1,8,128]{3,2,0,1:T(8,128)(2,1)}, bf16[1,1,8,128]{3,2,0,1:T(8,128)(2,1)S(1)}, u32[]{:S(2)}, u32[]{:S(2)}) collective-permute-start(bf16[1,1,8,128]{3,2,0,1:T(8,128)(2,1)} %get-tuple-element.24), channel_id=1, source_target_pairs={{0,8},{8,16},{16,24},{1,9},{9,17},{17,25},{2,10},{10,18},{18,26},{... | collective-permute-start | bytes 6152 | tf_op jit(solution)/shard_map/ppermute | solution.py:17
  13.0 1.3 %collective-permute-start.1 = (bf16[1,1,8,128]{3,2,1,0:T(8,128)(2,1)}, bf16[1,1,8,128]{3,2,1,0:T(8,128)(2,1)S(1)}, u32[]{:S(2)}, u32[]{:S(2)}) collective-permute-start(bf16[1,1,8,128]{3,2,1,0:T(8,128)(2,1)} %get-tuple-element.25), channel_id=1, source_target_pairs={{8,0},{16,8},{24,16},{9,1},{17,9},{25,17},{10,2},{18,10},{26,18},{... | collective-permute-start | bytes 6152 | tf_op jit(solution)/shard_map/ppermute | solution.py:19
  14.3 0.6 iota_compare_fusion.9
  14.9 0.7 select_convert_fusion.54
  15.7 0.8 constant_dynamic-slice_fusion
  16.5 2.2 %collective-permute-done.1 = bf16[1,1,8,128]{3,2,1,0:T(8,128)(2,1)S(1)} collective-permute-done((bf16[1,1,8,128]{3,2,1,0:T(8,128)(2,1)}, bf16[1,1,8,128]{3,2,1,0:T(8,128)(2,1)S(1)}, u32[]{:S(2)}, u32[]{:S(2)}) %collective-permute-start.1) | collective-permute-done | bytes 2080 | tf_op jit(solution)/shard_map/ppermute | solution.py:19
  18.7 1.3 %collective-permute-start.3 = (bf16[4,1,8,128]{3,2,0,1:T(8,128)(2,1)S(1)}, bf16[4,1,8,128]{3,2,0,1:T(8,128)(2,1)S(1)}, u32[]{:S(2)}, u32[]{:S(2)}) collective-permute-start(bf16[4,1,8,128]{3,2,0,1:T(8,128)(2,1)S(1)} %pad_maximum_fusion), channel_id=1, source_target_pairs={{4,0},{5,1},{6,2},{7,3},{12,8},{13,9},{14,10},{15,11},{20,16},{21,... | collective-permute-start | bytes 24584 | tf_op jit(solution)/shard_map/ppermute | solution.py:19
  20.0 4.5 %collective-permute-start.2 = (bf16[4,1,8,128]{3,2,0,1:T(8,128)(2,1)S(1)}, bf16[4,1,8,128]{3,2,0,1:T(8,128)(2,1)S(1)}, u32[]{:S(2)}, u32[]{:S(2)}) collective-permute-start(bf16[4,1,8,128]{3,2,0,1:T(8,128)(2,1)S(1)} %pad_maximum_fusion), channel_id=1, source_target_pairs={{0,4},{1,5},{2,6},{3,7},{8,12},{9,13},{10,14},{11,15},{16,20},{17,... | collective-permute-start | bytes 24584 | tf_op jit(solution)/shard_map/ppermute | solution.py:17
  24.6 1.3 %collective-permute-done.2 = bf16[4,1,8,128]{3,2,0,1:T(8,128)(2,1)S(1)} collective-permute-done((bf16[4,1,8,128]{3,2,0,1:T(8,128)(2,1)S(1)}, bf16[4,1,8,128]{3,2,0,1:T(8,128)(2,1)S(1)}, u32[]{:S(2)}, u32[]{:S(2)}) %collective-permute-start.2) | collective-permute-done | bytes 8224 | tf_op jit(solution)/shard_map/ppermute | solution.py:17
  26.9 0.2 fusion.21
  27.1 0.2 fusion.23
  27.5 0.2 fusion.27
  27.8 1.0 fusion.8
  28.8 5.1 %all_gather.16 = bf16[2,1,8,128]{3,0,1,2:T(2,128)(2,1)S(1)} all-gather(bf16[2,1,2,128]{3,0,1,2:T(2,128)(2,1)S(1)} %get-tuple-element.12), channel_id=1, replica_groups=mesh['gx'=4,'gy'=2,'gz'=4] {'gz'}, dimensions={2}, use_global_device_ids=true | all-gather | bytes 5120 | tf_op jit(solution)/shard_map/all_gather | solution.py:66
  34.1 3.5 %collective-permute-start.4 = (bf16[1,1,8,128]{3,2,0,1:T(8,128)(2,1)S(1)}, bf16[1,1,8,128]{3,2,0,1:T(8,128)(2,1)S(1)}, u32[]{:S(2)}, u32[]{:S(2)}) collective-permute-start(bf16[1,1,8,128]{3,2,0,1:T(8,128)(2,1)S(1)} %get-tuple-element.22), channel_id=1, source_target_pairs={{0,8},{8,16},{16,24},{1,9},{9,17},{17,25},{2,10},{10,18},{18,26},{... | collective-permute-start | bytes 6152 | tf_op jit(solution)/shard_map/ppermute | solution.py:17
  37.5 1.3 %collective-permute-start.5 = (bf16[1,1,8,128]{3,2,1,0:T(8,128)(2,1)S(1)}, bf16[1,1,8,128]{3,2,1,0:T(8,128)(2,1)S(1)}, u32[]{:S(2)}, u32[]{:S(2)}) collective-permute-start(bf16[1,1,8,128]{3,2,1,0:T(8,128)(2,1)S(1)} %get-tuple-element.23), channel_id=1, source_target_pairs={{8,0},{16,8},{24,16},{9,1},{17,9},{25,17},{10,2},{18,10},{26,18},{... | collective-permute-start | bytes 6152 | tf_op jit(solution)/shard_map/ppermute | solution.py:19
  38.8 4.2 %collective-permute-done.5 = bf16[1,1,8,128]{3,2,1,0:T(8,128)(2,1)S(1)} collective-permute-done((bf16[1,1,8,128]{3,2,1,0:T(8,128)(2,1)S(1)}, bf16[1,1,8,128]{3,2,1,0:T(8,128)(2,1)S(1)}, u32[]{:S(2)}, u32[]{:S(2)}) %collective-permute-start.5) | collective-permute-done | bytes 2080 | tf_op jit(solution)/shard_map/ppermute | solution.py:19
  43.0 1.3 %collective-permute-start.7 = (bf16[4,1,8,128]{3,2,0,1:T(8,128)(2,1)S(1)}, bf16[4,1,8,128]{3,2,0,1:T(8,128)(2,1)S(1)}, u32[]{:S(2)}, u32[]{:S(2)}) collective-permute-start(bf16[4,1,8,128]{3,2,0,1:T(8,128)(2,1)S(1)} %pad_maximum_fusion.1), channel_id=1, source_target_pairs={{4,0},{5,1},{6,2},{7,3},{12,8},{13,9},{14,10},{15,11},{20,16},{21,... | collective-permute-start | bytes 24584 | tf_op jit(solution)/shard_map/ppermute | solution.py:19
  44.3 4.5 %collective-permute-start.6 = (bf16[4,1,8,128]{3,2,0,1:T(8,128)(2,1)S(1)}, bf16[4,1,8,128]{3,2,0,1:T(8,128)(2,1)S(1)}, u32[]{:S(2)}, u32[]{:S(2)}) collective-permute-start(bf16[4,1,8,128]{3,2,0,1:T(8,128)(2,1)S(1)} %pad_maximum_fusion.1), channel_id=1, source_target_pairs={{0,4},{1,5},{2,6},{3,7},{8,12},{9,13},{10,14},{11,15},{16,20},{17,... | collective-permute-start | bytes 24584 | tf_op jit(solution)/shard_map/ppermute | solution.py:17
  48.9 1.3 %collective-permute-done.6 = bf16[4,1,8,128]{3,2,0,1:T(8,128)(2,1)S(1)} collective-permute-done((bf16[4,1,8,128]{3,2,0,1:T(8,128)(2,1)S(1)}, bf16[4,1,8,128]{3,2,0,1:T(8,128)(2,1)S(1)}, u32[]{:S(2)}, u32[]{:S(2)}) %collective-permute-start.6) | collective-permute-done | bytes 8224 | tf_op jit(solution)/shard_map/ppermute | solution.py:17
  51.2 0.2 fusion.39
  51.6 0.2 fusion.43
  51.8 0.2 fusion.45
  52.1 1.0 fusion.6
  53.2 5.1 %all_gather.17 = bf16[2,1,8,128]{3,0,1,2:T(2,128)(2,1)S(1)} all-gather(bf16[2,1,2,128]{3,0,1,2:T(2,128)(2,1)S(1)} %get-tuple-element.10), channel_id=1, replica_groups=mesh['gx'=4,'gy'=2,'gz'=4] {'gz'}, dimensions={2}, use_global_device_ids=true | all-gather | bytes 5120 | tf_op jit(solution)/shard_map/all_gather | solution.py:66
  58.4 3.5 %collective-permute-start.8 = (bf16[1,1,8,128]{3,2,0,1:T(8,128)(2,1)S(1)}, bf16[1,1,8,128]{3,2,0,1:T(8,128)(2,1)S(1)}, u32[]{:S(2)}, u32[]{:S(2)}) collective-permute-start(bf16[1,1,8,128]{3,2,0,1:T(8,128)(2,1)S(1)} %get-tuple-element.20), channel_id=1, source_target_pairs={{0,8},{8,16},{16,24},{1,9},{9,17},{17,25},{2,10},{10,18},{18,26},{... | collective-permute-start | bytes 6152 | tf_op jit(solution)/shard_map/ppermute | solution.py:17
  61.8 1.3 %collective-permute-start.9 = (bf16[1,1,8,128]{3,2,1,0:T(8,128)(2,1)S(1)}, bf16[1,1,8,128]{3,2,1,0:T(8,128)(2,1)S(1)}, u32[]{:S(2)}, u32[]{:S(2)}) collective-permute-start(bf16[1,1,8,128]{3,2,1,0:T(8,128)(2,1)S(1)} %get-tuple-element.21), channel_id=1, source_target_pairs={{8,0},{16,8},{24,16},{9,1},{17,9},{25,17},{10,2},{18,10},{26,18},{... | collective-permute-start | bytes 6152 | tf_op jit(solution)/shard_map/ppermute | solution.py:19
  63.1 4.2 %collective-permute-done.9 = bf16[1,1,8,128]{3,2,1,0:T(8,128)(2,1)S(1)} collective-permute-done((bf16[1,1,8,128]{3,2,1,0:T(8,128)(2,1)S(1)}, bf16[1,1,8,128]{3,2,1,0:T(8,128)(2,1)S(1)}, u32[]{:S(2)}, u32[]{:S(2)}) %collective-permute-start.9) | collective-permute-done | bytes 2080 | tf_op jit(solution)/shard_map/ppermute | solution.py:19
  67.3 1.3 %collective-permute-start.11 = (bf16[4,1,8,128]{3,2,0,1:T(8,128)(2,1)S(1)}, bf16[4,1,8,128]{3,2,0,1:T(8,128)(2,1)S(1)}, u32[]{:S(2)}, u32[]{:S(2)}) collective-permute-start(bf16[4,1,8,128]{3,2,0,1:T(8,128)(2,1)S(1)} %pad_maximum_fusion.2), channel_id=1, source_target_pairs={{4,0},{5,1},{6,2},{7,3},{12,8},{13,9},{14,10},{15,11},{20,16},{21,... | collective-permute-start | bytes 24584 | tf_op jit(solution)/shard_map/ppermute | solution.py:19
  68.6 4.5 %collective-permute-start.10 = (bf16[4,1,8,128]{3,2,0,1:T(8,128)(2,1)S(1)}, bf16[4,1,8,128]{3,2,0,1:T(8,128)(2,1)S(1)}, u32[]{:S(2)}, u32[]{:S(2)}) collective-permute-start(bf16[4,1,8,128]{3,2,0,1:T(8,128)(2,1)S(1)} %pad_maximum_fusion.2), channel_id=1, source_target_pairs={{0,4},{1,5},{2,6},{3,7},{8,12},{9,13},{10,14},{11,15},{16,20},{17,... | collective-permute-start | bytes 24584 | tf_op jit(solution)/shard_map/ppermute | solution.py:17
  73.2 1.3 %collective-permute-done.10 = bf16[4,1,8,128]{3,2,0,1:T(8,128)(2,1)S(1)} collective-permute-done((bf16[4,1,8,128]{3,2,0,1:T(8,128)(2,1)S(1)}, bf16[4,1,8,128]{3,2,0,1:T(8,128)(2,1)S(1)}, u32[]{:S(2)}, u32[]{:S(2)}) %collective-permute-start.10) | collective-permute-done | bytes 8224 | tf_op jit(solution)/shard_map/ppermute | solution.py:17
  75.5 0.2 fusion.57
  75.7 0.2 fusion.59
  75.9 0.2 fusion.61
  76.2 0.2 fusion.63
  76.4 1.0 fusion.4
  77.5 5.1 %all_gather.18 = bf16[2,1,8,128]{3,0,1,2:T(2,128)(2,1)S(1)} all-gather(bf16[2,1,2,128]{3,0,1,2:T(2,128)(2,1)S(1)} %get-tuple-element.8), channel_id=1, replica_groups=mesh['gx'=4,'gy'=2,'gz'=4] {'gz'}, dimensions={2}, use_global_device_ids=true | all-gather | bytes 5120 | tf_op jit(solution)/shard_map/all_gather | solution.py:66
  82.7 2.3 %collective-permute-start.12 = (bf16[1,1,8,128]{3,2,0,1:T(8,128)(2,1)S(1)}, bf16[1,1,8,128]{3,2,0,1:T(8,128)(2,1)S(1)}, u32[]{:S(2)}, u32[]{:S(2)}) collective-permute-start(bf16[1,1,8,128]{3,2,0,1:T(8,128)(2,1)S(1)} %get-tuple-element.18), channel_id=1, source_target_pairs={{0,8},{8,16},{16,24},{1,9},{9,17},{17,25},{2,10},{10,18},{18,26},{... | collective-permute-start | bytes 6152 | tf_op jit(solution)/shard_map/ppermute | solution.py:17
  85.0 1.3 %collective-permute-start.13 = (bf16[1,1,8,128]{3,2,1,0:T(8,128)(2,1)S(1)}, bf16[1,1,8,128]{3,2,1,0:T(8,128)(2,1)S(1)}, u32[]{:S(2)}, u32[]{:S(2)}) collective-permute-start(bf16[1,1,8,128]{3,2,1,0:T(8,128)(2,1)S(1)} %get-tuple-element.19), channel_id=1, source_target_pairs={{8,0},{16,8},{24,16},{9,1},{17,9},{25,17},{10,2},{18,10},{26,18},{... | collective-permute-start | bytes 6152 | tf_op jit(solution)/shard_map/ppermute | solution.py:19
  86.3 4.2 %collective-permute-done.13 = bf16[1,1,8,128]{3,2,1,0:T(8,128)(2,1)S(1)} collective-permute-done((bf16[1,1,8,128]{3,2,1,0:T(8,128)(2,1)S(1)}, bf16[1,1,8,128]{3,2,1,0:T(8,128)(2,1)S(1)}, u32[]{:S(2)}, u32[]{:S(2)}) %collective-permute-start.13) | collective-permute-done | bytes 2080 | tf_op jit(solution)/shard_map/ppermute | solution.py:19
  90.5 1.3 %collective-permute-start.15 = (bf16[4,1,8,128]{3,2,0,1:T(8,128)(2,1)S(1)}, bf16[4,1,8,128]{3,2,0,1:T(8,128)(2,1)S(1)}, u32[]{:S(2)}, u32[]{:S(2)}) collective-permute-start(bf16[4,1,8,128]{3,2,0,1:T(8,128)(2,1)S(1)} %pad_maximum_fusion.3), channel_id=1, source_target_pairs={{4,0},{5,1},{6,2},{7,3},{12,8},{13,9},{14,10},{15,11},{20,16},{21,... | collective-permute-start | bytes 24584 | tf_op jit(solution)/shard_map/ppermute | solution.py:19
  91.8 4.5 %collective-permute-start.14 = (bf16[4,1,8,128]{3,2,0,1:T(8,128)(2,1)S(1)}, bf16[4,1,8,128]{3,2,0,1:T(8,128)(2,1)S(1)}, u32[]{:S(2)}, u32[]{:S(2)}) collective-permute-start(bf16[4,1,8,128]{3,2,0,1:T(8,128)(2,1)S(1)} %pad_maximum_fusion.3), channel_id=1, source_target_pairs={{0,4},{1,5},{2,6},{3,7},{8,12},{9,13},{10,14},{11,15},{16,20},{17,... | collective-permute-start | bytes 24584 | tf_op jit(solution)/shard_map/ppermute | solution.py:17
  96.3 1.3 %collective-permute-done.14 = bf16[4,1,8,128]{3,2,0,1:T(8,128)(2,1)S(1)} collective-permute-done((bf16[4,1,8,128]{3,2,0,1:T(8,128)(2,1)S(1)}, bf16[4,1,8,128]{3,2,0,1:T(8,128)(2,1)S(1)}, u32[]{:S(2)}, u32[]{:S(2)}) %collective-permute-start.14) | collective-permute-done | bytes 8224 | tf_op jit(solution)/shard_map/ppermute | solution.py:17
  98.7 0.2 fusion.75
  99.1 0.2 fusion.79
  99.3 0.2 fusion.81
  99.5 1.0 fusion.2
  100.6 5.1 %all_gather.19 = bf16[2,1,8,128]{3,0,1,2:T(2,128)(2,1)S(1)} all-gather(bf16[2,1,2,128]{3,0,1,2:T(2,128)(2,1)S(1)} %get-tuple-element.14), channel_id=1, replica_groups=mesh['gx'=4,'gy'=2,'gz'=4] {'gz'}, dimensions={2}, use_global_device_ids=true | all-gather | bytes 5120 | tf_op jit(solution)/shard_map/all_gather | solution.py:66
  105.8 1.9 %collective-permute-start.16 = (bf16[1,1,8,128]{3,2,0,1:T(8,128)(2,1)S(1)}, bf16[1,1,8,128]{3,2,0,1:T(8,128)(2,1)S(1)}, u32[]{:S(2)}, u32[]{:S(2)}) collective-permute-start(bf16[1,1,8,128]{3,2,0,1:T(8,128)(2,1)S(1)} %get-tuple-element.16), channel_id=1, source_target_pairs={{0,8},{8,16},{16,24},{1,9},{9,17},{17,25},{2,10},{10,18},{18,26},{... | collective-permute-start | bytes 6152 | tf_op jit(solution)/shard_map/ppermute | solution.py:17
  107.7 1.3 %collective-permute-start.17 = (bf16[1,1,8,128]{3,2,1,0:T(8,128)(2,1)S(1)}, bf16[1,1,8,128]{3,2,1,0:T(8,128)(2,1)S(1)}, u32[]{:S(2)}, u32[]{:S(2)}) collective-permute-start(bf16[1,1,8,128]{3,2,1,0:T(8,128)(2,1)S(1)} %get-tuple-element.17), channel_id=1, source_target_pairs={{8,0},{16,8},{24,16},{9,1},{17,9},{25,17},{10,2},{18,10},{26,18},{... | collective-permute-start | bytes 6152 | tf_op jit(solution)/shard_map/ppermute | solution.py:19
  109.0 4.2 %collective-permute-done.17 = bf16[1,1,8,128]{3,2,1,0:T(8,128)(2,1)S(1)} collective-permute-done((bf16[1,1,8,128]{3,2,1,0:T(8,128)(2,1)S(1)}, bf16[1,1,8,128]{3,2,1,0:T(8,128)(2,1)S(1)}, u32[]{:S(2)}, u32[]{:S(2)}) %collective-permute-start.17) | collective-permute-done | bytes 2080 | tf_op jit(solution)/shard_map/ppermute | solution.py:19
  113.2 1.3 %collective-permute-start.19 = (bf16[4,1,8,128]{3,2,0,1:T(8,128)(2,1)S(1)}, bf16[4,1,8,128]{3,2,0,1:T(8,128)(2,1)S(1)}, u32[]{:S(2)}, u32[]{:S(2)}) collective-permute-start(bf16[4,1,8,128]{3,2,0,1:T(8,128)(2,1)S(1)} %pad_maximum_fusion.4), channel_id=1, source_target_pairs={{4,0},{5,1},{6,2},{7,3},{12,8},{13,9},{14,10},{15,11},{20,16},{21,... | collective-permute-start | bytes 24584 | tf_op jit(solution)/shard_map/ppermute | solution.py:19
  114.5 4.5 %collective-permute-start.18 = (bf16[4,1,8,128]{3,2,0,1:T(8,128)(2,1)S(1)}, bf16[4,1,8,128]{3,2,0,1:T(8,128)(2,1)S(1)}, u32[]{:S(2)}, u32[]{:S(2)}) collective-permute-start(bf16[4,1,8,128]{3,2,0,1:T(8,128)(2,1)S(1)} %pad_maximum_fusion.4), channel_id=1, source_target_pairs={{0,4},{1,5},{2,6},{3,7},{8,12},{9,13},{10,14},{11,15},{16,20},{17,... | collective-permute-start | bytes 24584 | tf_op jit(solution)/shard_map/ppermute | solution.py:17
  119.1 0.6 copy.50
  119.6 0.8 collective-permute-done.18
  121.4 0.2 fusion.93
  121.8 0.2 fusion.97
  122.1 0.2 fusion.99
  122.3 1.0 fusion
  123.3 0.6 copy.51
  (77 shorter events, 6.9 us)
Async XLA Ops:
  0.6 27.2 %copy-start = (bf16[2,1,2,27,128,128]{5,4,3,2,1,0:T(8,128)(2,1)S(1)}, bf16[2,1,2,27,128,128]{5,4,3,2,1,0:T(8,128)(2,1)}, u32[]{:S(2)}) copy-start(bf16[2,1,2,27,128,128]{5,4,3,2,1,0:T(8,128)(2,1)} %param.5) | copy-start | bytes 10616836
  0.6 33.3 %copy-start.1 = (s32[2,1,8]{2,1,0:T(1,128)S(1)}, s32[2,1,8]{2,1,0:T(1,128)}, u32[]{:S(2)}) copy-start(s32[2,1,8]{2,1,0:T(1,128)} %param.7) | copy-start | bytes 196
  9.0 7.5 %collective-permute-start = (bf16[1,1,8,128]{3,2,0,1:T(8,128)(2,1)}, bf16[1,1,8,128]{3,2,0,1:T(8,128)(2,1)S(1)}, u32[]{:S(2)}, u32[]{:S(2)}) collective-permute-start(bf16[1,1,8,128]{3,2,0,1:T(8,128)(2,1)} %get-tuple-element.24), channel_id=1, source_target_pairs={{0,8},{8,16},{16,24},{1,9},{9,17},{17,25},{2,10},{10,18},{18,26},{... | collective-permute-start | bytes 6152 | tf_op jit(solution)/shard_map/ppermute | solution.py:17
  13.0 5.7 %collective-permute-start.1 = (bf16[1,1,8,128]{3,2,1,0:T(8,128)(2,1)}, bf16[1,1,8,128]{3,2,1,0:T(8,128)(2,1)S(1)}, u32[]{:S(2)}, u32[]{:S(2)}) collective-permute-start(bf16[1,1,8,128]{3,2,1,0:T(8,128)(2,1)} %get-tuple-element.25), channel_id=1, source_target_pairs={{8,0},{16,8},{24,16},{9,1},{17,9},{25,17},{10,2},{18,10},{26,18},{... | collective-permute-start | bytes 6152 | tf_op jit(solution)/shard_map/ppermute | solution.py:19
  14.9 13.9 %copy-start.3 = (f32[2,1,2,128]{3,2,1,0:T(2,128)S(1)}, f32[2,1,2,128]{3,2,1,0:T(2,128)}, u32[]{:S(2)}) copy-start(f32[2,1,2,128]{3,2,1,0:T(2,128)} %param.9) | copy-start | bytes 6148
  18.7 5.9 %collective-permute-start.3 = (bf16[4,1,8,128]{3,2,0,1:T(8,128)(2,1)S(1)}, bf16[4,1,8,128]{3,2,0,1:T(8,128)(2,1)S(1)}, u32[]{:S(2)}, u32[]{:S(2)}) collective-permute-start(bf16[4,1,8,128]{3,2,0,1:T(8,128)(2,1)S(1)} %pad_maximum_fusion), channel_id=1, source_target_pairs={{4,0},{5,1},{6,2},{7,3},{12,8},{13,9},{14,10},{15,11},{20,16},{21,... | collective-permute-start | bytes 24584 | tf_op jit(solution)/shard_map/ppermute | solution.py:19
  20.0 5.9 %collective-permute-start.2 = (bf16[4,1,8,128]{3,2,0,1:T(8,128)(2,1)S(1)}, bf16[4,1,8,128]{3,2,0,1:T(8,128)(2,1)S(1)}, u32[]{:S(2)}, u32[]{:S(2)}) collective-permute-start(bf16[4,1,8,128]{3,2,0,1:T(8,128)(2,1)S(1)} %pad_maximum_fusion), channel_id=1, source_target_pairs={{0,4},{1,5},{2,6},{3,7},{8,12},{9,13},{10,14},{11,15},{16,20},{17,... | collective-permute-start | bytes 24584 | tf_op jit(solution)/shard_map/ppermute | solution.py:17
  34.1 4.8 %collective-permute-start.4 = (bf16[1,1,8,128]{3,2,0,1:T(8,128)(2,1)S(1)}, bf16[1,1,8,128]{3,2,0,1:T(8,128)(2,1)S(1)}, u32[]{:S(2)}, u32[]{:S(2)}) collective-permute-start(bf16[1,1,8,128]{3,2,0,1:T(8,128)(2,1)S(1)} %get-tuple-element.22), channel_id=1, source_target_pairs={{0,8},{8,16},{16,24},{1,9},{9,17},{17,25},{2,10},{10,18},{18,26},{... | collective-permute-start | bytes 6152 | tf_op jit(solution)/shard_map/ppermute | solution.py:17
  37.5 5.5 %collective-permute-start.5 = (bf16[1,1,8,128]{3,2,1,0:T(8,128)(2,1)S(1)}, bf16[1,1,8,128]{3,2,1,0:T(8,128)(2,1)S(1)}, u32[]{:S(2)}, u32[]{:S(2)}) collective-permute-start(bf16[1,1,8,128]{3,2,1,0:T(8,128)(2,1)S(1)} %get-tuple-element.23), channel_id=1, source_target_pairs={{8,0},{16,8},{24,16},{9,1},{17,9},{25,17},{10,2},{18,10},{26,18},{... | collective-permute-start | bytes 6152 | tf_op jit(solution)/shard_map/ppermute | solution.py:19
  43.0 5.8 %collective-permute-start.7 = (bf16[4,1,8,128]{3,2,0,1:T(8,128)(2,1)S(1)}, bf16[4,1,8,128]{3,2,0,1:T(8,128)(2,1)S(1)}, u32[]{:S(2)}, u32[]{:S(2)}) collective-permute-start(bf16[4,1,8,128]{3,2,0,1:T(8,128)(2,1)S(1)} %pad_maximum_fusion.1), channel_id=1, source_target_pairs={{4,0},{5,1},{6,2},{7,3},{12,8},{13,9},{14,10},{15,11},{20,16},{21,... | collective-permute-start | bytes 24584 | tf_op jit(solution)/shard_map/ppermute | solution.py:19
  44.3 5.9 %collective-permute-start.6 = (bf16[4,1,8,128]{3,2,0,1:T(8,128)(2,1)S(1)}, bf16[4,1,8,128]{3,2,0,1:T(8,128)(2,1)S(1)}, u32[]{:S(2)}, u32[]{:S(2)}) collective-permute-start(bf16[4,1,8,128]{3,2,0,1:T(8,128)(2,1)S(1)} %pad_maximum_fusion.1), channel_id=1, source_target_pairs={{0,4},{1,5},{2,6},{3,7},{8,12},{9,13},{10,14},{11,15},{16,20},{17,... | collective-permute-start | bytes 24584 | tf_op jit(solution)/shard_map/ppermute | solution.py:17
  58.4 4.8 %collective-permute-start.8 = (bf16[1,1,8,128]{3,2,0,1:T(8,128)(2,1)S(1)}, bf16[1,1,8,128]{3,2,0,1:T(8,128)(2,1)S(1)}, u32[]{:S(2)}, u32[]{:S(2)}) collective-permute-start(bf16[1,1,8,128]{3,2,0,1:T(8,128)(2,1)S(1)} %get-tuple-element.20), channel_id=1, source_target_pairs={{0,8},{8,16},{16,24},{1,9},{9,17},{17,25},{2,10},{10,18},{18,26},{... | collective-permute-start | bytes 6152 | tf_op jit(solution)/shard_map/ppermute | solution.py:17
  61.8 5.5 %collective-permute-start.9 = (bf16[1,1,8,128]{3,2,1,0:T(8,128)(2,1)S(1)}, bf16[1,1,8,128]{3,2,1,0:T(8,128)(2,1)S(1)}, u32[]{:S(2)}, u32[]{:S(2)}) collective-permute-start(bf16[1,1,8,128]{3,2,1,0:T(8,128)(2,1)S(1)} %get-tuple-element.21), channel_id=1, source_target_pairs={{8,0},{16,8},{24,16},{9,1},{17,9},{25,17},{10,2},{18,10},{26,18},{... | collective-permute-start | bytes 6152 | tf_op jit(solution)/shard_map/ppermute | solution.py:19
  67.3 5.8 %collective-permute-start.11 = (bf16[4,1,8,128]{3,2,0,1:T(8,128)(2,1)S(1)}, bf16[4,1,8,128]{3,2,0,1:T(8,128)(2,1)S(1)}, u32[]{:S(2)}, u32[]{:S(2)}) collective-permute-start(bf16[4,1,8,128]{3,2,0,1:T(8,128)(2,1)S(1)} %pad_maximum_fusion.2), channel_id=1, source_target_pairs={{4,0},{5,1},{6,2},{7,3},{12,8},{13,9},{14,10},{15,11},{20,16},{21,... | collective-permute-start | bytes 24584 | tf_op jit(solution)/shard_map/ppermute | solution.py:19
  68.6 5.9 %collective-permute-start.10 = (bf16[4,1,8,128]{3,2,0,1:T(8,128)(2,1)S(1)}, bf16[4,1,8,128]{3,2,0,1:T(8,128)(2,1)S(1)}, u32[]{:S(2)}, u32[]{:S(2)}) collective-permute-start(bf16[4,1,8,128]{3,2,0,1:T(8,128)(2,1)S(1)} %pad_maximum_fusion.2), channel_id=1, source_target_pairs={{0,4},{1,5},{2,6},{3,7},{8,12},{9,13},{10,14},{11,15},{16,20},{17,... | collective-permute-start | bytes 24584 | tf_op jit(solution)/shard_map/ppermute | solution.py:17
  77.4 23.2 %copy-start.2 = (f32[2,1,2,128]{3,2,1,0:T(2,128)S(1)}, f32[2,1,2,128]{3,2,1,0:T(2,128)}, u32[]{:S(2)}) copy-start(f32[2,1,2,128]{3,2,1,0:T(2,128)} %param.8) | copy-start | bytes 6148
  82.7 3.6 %collective-permute-start.12 = (bf16[1,1,8,128]{3,2,0,1:T(8,128)(2,1)S(1)}, bf16[1,1,8,128]{3,2,0,1:T(8,128)(2,1)S(1)}, u32[]{:S(2)}, u32[]{:S(2)}) collective-permute-start(bf16[1,1,8,128]{3,2,0,1:T(8,128)(2,1)S(1)} %get-tuple-element.18), channel_id=1, source_target_pairs={{0,8},{8,16},{16,24},{1,9},{9,17},{17,25},{2,10},{10,18},{18,26},{... | collective-permute-start | bytes 6152 | tf_op jit(solution)/shard_map/ppermute | solution.py:17
  85.0 5.5 %collective-permute-start.13 = (bf16[1,1,8,128]{3,2,1,0:T(8,128)(2,1)S(1)}, bf16[1,1,8,128]{3,2,1,0:T(8,128)(2,1)S(1)}, u32[]{:S(2)}, u32[]{:S(2)}) collective-permute-start(bf16[1,1,8,128]{3,2,1,0:T(8,128)(2,1)S(1)} %get-tuple-element.19), channel_id=1, source_target_pairs={{8,0},{16,8},{24,16},{9,1},{17,9},{25,17},{10,2},{18,10},{26,18},{... | collective-permute-start | bytes 6152 | tf_op jit(solution)/shard_map/ppermute | solution.py:19
  90.5 5.8 %collective-permute-start.15 = (bf16[4,1,8,128]{3,2,0,1:T(8,128)(2,1)S(1)}, bf16[4,1,8,128]{3,2,0,1:T(8,128)(2,1)S(1)}, u32[]{:S(2)}, u32[]{:S(2)}) collective-permute-start(bf16[4,1,8,128]{3,2,0,1:T(8,128)(2,1)S(1)} %pad_maximum_fusion.3), channel_id=1, source_target_pairs={{4,0},{5,1},{6,2},{7,3},{12,8},{13,9},{14,10},{15,11},{20,16},{21,... | collective-permute-start | bytes 24584 | tf_op jit(solution)/shard_map/ppermute | solution.py:19
  91.8 5.9 %collective-permute-start.14 = (bf16[4,1,8,128]{3,2,0,1:T(8,128)(2,1)S(1)}, bf16[4,1,8,128]{3,2,0,1:T(8,128)(2,1)S(1)}, u32[]{:S(2)}, u32[]{:S(2)}) collective-permute-start(bf16[4,1,8,128]{3,2,0,1:T(8,128)(2,1)S(1)} %pad_maximum_fusion.3), channel_id=1, source_target_pairs={{0,4},{1,5},{2,6},{3,7},{8,12},{9,13},{10,14},{11,15},{16,20},{17,... | collective-permute-start | bytes 24584 | tf_op jit(solution)/shard_map/ppermute | solution.py:17
  105.8 3.2 %collective-permute-start.16 = (bf16[1,1,8,128]{3,2,0,1:T(8,128)(2,1)S(1)}, bf16[1,1,8,128]{3,2,0,1:T(8,128)(2,1)S(1)}, u32[]{:S(2)}, u32[]{:S(2)}) collective-permute-start(bf16[1,1,8,128]{3,2,0,1:T(8,128)(2,1)S(1)} %get-tuple-element.16), channel_id=1, source_target_pairs={{0,8},{8,16},{16,24},{1,9},{9,17},{17,25},{2,10},{10,18},{18,26},{... | collective-permute-start | bytes 6152 | tf_op jit(solution)/shard_map/ppermute | solution.py:17
  107.7 5.5 %collective-permute-start.17 = (bf16[1,1,8,128]{3,2,1,0:T(8,128)(2,1)S(1)}, bf16[1,1,8,128]{3,2,1,0:T(8,128)(2,1)S(1)}, u32[]{:S(2)}, u32[]{:S(2)}) collective-permute-start(bf16[1,1,8,128]{3,2,1,0:T(8,128)(2,1)S(1)} %get-tuple-element.17), channel_id=1, source_target_pairs={{8,0},{16,8},{24,16},{9,1},{17,9},{25,17},{10,2},{18,10},{26,18},{... | collective-permute-start | bytes 6152 | tf_op jit(solution)/shard_map/ppermute | solution.py:19
  113.2 6.4 %collective-permute-start.19 = (bf16[4,1,8,128]{3,2,0,1:T(8,128)(2,1)S(1)}, bf16[4,1,8,128]{3,2,0,1:T(8,128)(2,1)S(1)}, u32[]{:S(2)}, u32[]{:S(2)}) collective-permute-start(bf16[4,1,8,128]{3,2,0,1:T(8,128)(2,1)S(1)} %pad_maximum_fusion.4), channel_id=1, source_target_pairs={{4,0},{5,1},{6,2},{7,3},{12,8},{13,9},{14,10},{15,11},{20,16},{21,... | collective-permute-start | bytes 24584 | tf_op jit(solution)/shard_map/ppermute | solution.py:19
  114.5 5.9 %collective-permute-start.18 = (bf16[4,1,8,128]{3,2,0,1:T(8,128)(2,1)S(1)}, bf16[4,1,8,128]{3,2,0,1:T(8,128)(2,1)S(1)}, u32[]{:S(2)}, u32[]{:S(2)}) collective-permute-start(bf16[4,1,8,128]{3,2,0,1:T(8,128)(2,1)S(1)} %pad_maximum_fusion.4), channel_id=1, source_target_pairs={{0,4},{1,5},{2,6},{3,7},{8,12},{9,13},{10,14},{11,15},{16,20},{17,... | collective-permute-start | bytes 24584 | tf_op jit(solution)/shard_map/ppermute | solution.py:17
where the time goes:
time: 125 us; the launch traced here: 124 us
  starting transfers between devices  50.7 us (41%)
  blocking collectives  26.4 us (21%)
  waiting for transfers between devices  25 us (20%)
  matrix products  15.5 us (12%)
  local copies, waits for them, and re-layouts  3.64 us (3%)
  other arithmetic  1.62 us (1%)
    ppermute x10, starting transfers between devices, padded_2(): lax.ppermute(tail, axis, [(i, (i + 1) % count) for i in range(ends)])  37.9 us
    all_gather x5, blocking collectives, operator(): lax.all_gather(vector.astype(jnp.bfloat16), 'gz', axis=2, tiled=True)  26.4 us
    ppermute x10, waiting for transfers between devices, padded_2(): lax.ppermute(head, axis, [((i + 1) % count, i) for i in range(ends)])  18.9 us
    ppermute x10, starting transfers between devices, padded_2(): lax.ppermute(head, axis, [((i + 1) % count, i) for i in range(ends)])  12.9 us
    dot_general x45, matrix products, coupled_product(): jnp.einsum('xyscp,xypw->xyscw', table, column, preferred_element_type=jnp...  9.05 us
    ppermute x10, waiting for transfers between devices, padded_2(): lax.ppermute(tail, axis, [(i, (i + 1) % count) for i in range(ends)])  6.07 us
    dot_general x5, matrix products, coupled_product(): jnp.einsum('xysoj,xysoij->xysi', gathered, matrix, preferred_element_type...  5.22 us
  transfers between devices with their start and end apart: 20, of which 10 were waited for; matrix products, arithmetic and copies ran while one was open for 2% of the time, Pallas kernels for 0%

commit v1 on v0

v1 whole, which is shorter than its diff:
```python
import functools

import jax
import jax.numpy as jnp
from jax import lax
from jax.experimental import pallas as pl
from jax.experimental.pallas import tpu as pltpu
from jax.sharding import PartitionSpec as P

DEG = 4
CENTER = 1.0
SPREAD = 0.8
LANES = 128
GRANT = 16 * 2**20
AXES = ("gx", "gy", "gz")
VMEM = pl.BlockSpec(memory_space=pltpu.VMEM)
SMEM = pl.BlockSpec(memory_space=pltpu.SMEM)


def split(value, count):
    if count & (count - 1) == 0:
        shift = count.bit_length() - 1
        return value >> shift, value & (count - 1)
    whole = jnp.floor((value.astype(jnp.float32) + 0.5) * (1.0 / count)).astype(jnp.int32)
    return whole, value - whole * count


class Plan:
    def __init__(self, axis_sizes, local_shape):
        self.gx, self.gy, self.gz = axis_sizes
        self.nx, self.ny, self.nz, self.width = local_shape
        self.devices = self.gx * self.gy * self.gz
        self.rows = self.nx * self.ny * self.nz
        self.sent = 2 * self.rows
        self.sources = self.devices * self.sent
        self.few = self.ny == 1 and self.gy <= 2
        self.spans = min(3, self.gy) if self.few else 3
        self.entries = 9 * self.spans
        self.pitch = 32
        self.targets = -(-self.rows * self.pitch // LANES) * LANES

    def first_span(self):
        if not self.few:
            return 0
        return 1 - lax.axis_index("gy")

    def offsets(self, entry):
        return entry // (3 * self.spans), entry // 3 % self.spans, entry % 3

    def place(self, row):
        return row // (self.ny * self.nz), row // self.nz % self.ny, row % self.nz


def send(plan, vector, tail, pay_ref):
    tile = jnp.concatenate([vector, tail], axis=0).astype(jnp.bfloat16)
    pay_ref[...] = jnp.broadcast_to(tile[None], pay_ref.shape)


def first_kernel(plan, order_ref, start_ref, pay_ref):
    first = lax.axis_index("gz") * plan.nz
    planes = []
    for row in range(plan.rows):
        x, y, s = plan.place(row)
        planes.append(jnp.full((1, plan.width), order_ref[x, y, first + s], jnp.int32))
    planes = jnp.concatenate(planes, axis=0).astype(jnp.float32)
    send(plan, start_ref[...], planes, pay_ref)


def selection(plan, received_ref, order_ref, pattern_ref, select_ref):
    first = lax.axis_index("gz") * plan.nz
    lane = lax.broadcasted_iota(jnp.int32, (1, plan.targets), 1)
    row, entry = split(lane, plan.pitch)
    a, rest = split(entry, 3 * plan.spans)
    b, c = split(rest, 3)
    b = b + plan.first_span()
    plane = jnp.zeros_like(lane)
    keep = jnp.zeros_like(lane)
    for number in range(plan.rows):
        x, y, s = plan.place(number)
        plane = jnp.where(row == number, order_ref[x, y, first + s], plane)
        present = pattern_ref[x, y, pl.ds(first + s, 1), :]
        for index in range(plan.entries):
            i, j, k = plan.offsets(index)
            here = lane == number * plan.pitch + index
            if (i, k) == (1, 1):
                value = jnp.where(j + plan.first_span() == 1, 1, 0)
            else:
                value = 0
            for span in range(3):
                entry_of = 9 * i + 3 * span + k
                flag = present[:, entry_of : entry_of + 1]
                if entry_of == 13:
                    flag = jnp.ones_like(flag)
                match = j + plan.first_span() == span
                keep = jnp.where(here & match, flag, keep)
    x, y, s = row, row, row
    xy, s = split(row, plan.nz)
    x, y = split(xy, plan.ny)
    want_x = lax.axis_index("gx") * plan.nx + x + a - 1
    want_y = lax.axis_index("gy") * plan.ny + y + b - 1
    want_z = plane + c - 1
    keep = jnp.where((keep > 0) & (entry < plan.entries) & (row < plan.rows), 1, 0)

    source = lax.broadcasted_iota(jnp.int32, (plan.sources, LANES), 0)
    device, rank = split(source, plan.sent)
    device_xy, _ = split(device, plan.gz)
    device_x, device_y = split(device_xy, plan.gy)
    rank_xy, _ = split(rank, plan.nz)
    rank_x, rank_y = split(rank_xy, plan.ny)
    has_x = device_x * plan.nx + rank_x
    has_y = device_y * plan.ny + rank_y
    values = received_ref[...].astype(jnp.float32)
    has_z = pltpu.roll(values, plan.sources - plan.rows, 0).astype(jnp.int32)
    for block in range(plan.targets // LANES):
        part = slice(block * LANES, (block + 1) * LANES)
        hit = (has_x == want_x[:, part]) & (has_y == want_y[:, part]) & (has_z[:, :LANES] == want_z[:, part])
        hit = hit & (rank < plan.rows) & (keep[:, part] > 0)
        table = jnp.where(hit, 1.0, 0.0)
        select_ref[part, :] = table.T.astype(jnp.bfloat16)


def product(plan, blocks_ref, received_ref, select_ref, gather_ref, result_ref):
    gather_ref[...] = jnp.dot(
        select_ref[...], received_ref[...], preferred_element_type=jnp.float32
    )
    span = plan.first_span()
    size = plan.width
    lane = lax.broadcasted_iota(jnp.int32, (size, size), 1)
    line = lax.broadcasted_iota(jnp.int32, (size, size), 0)
    for row in range(plan.rows):
        x, y, s = plan.place(row)
        total = jnp.zeros((size, size), jnp.float32)
        for entry in range(plan.entries):
            i, j, k = plan.offsets(entry)
            at = row * plan.pitch + entry
            block = blocks_ref[x, y, s, 9 * i + 3 * (j + span) + k].astype(jnp.float32)
            total = total + block * gather_ref[at : at + 1, :]
        sums = jnp.sum(total, axis=1, keepdims=True)
        line_sums = jnp.where(lane == line, sums, 0.0)
        result_ref[row : row + 1, :] = jnp.sum(line_sums, axis=0, keepdims=True)


def opening_kernel(
    plan, received_ref, blocks_ref, order_ref, pattern_ref, start_ref, rhs_ref,
    pay_ref, select_ref, smoothed_ref, remainder_ref, search_ref, gather_ref, result_ref,
):
    selection(plan, received_ref, order_ref, pattern_ref, select_ref)
    product(plan, blocks_ref, received_ref, select_ref, gather_ref, result_ref)
    remainder = rhs_ref[...] - result_ref[...]
    search = remainder / CENTER
    send(plan, search, jnp.zeros_like(search), pay_ref)
    remainder_ref[...] = remainder
    search_ref[...] = search
    smoothed_ref[...] = start_ref[...] + search


def turn_kernel(
    plan, factors, received_ref, blocks_ref, select_ref, smoothed_in, remainder_in, search_in,
    pay_ref, smoothed_ref, remainder_ref, search_ref, gather_ref, result_ref,
):
    product(plan, blocks_ref, received_ref, select_ref, gather_ref, result_ref)
    remainder = remainder_in[...] - result_ref[...]
    search = factors[0] * search_in[...] + factors[1] * remainder
    send(plan, search, jnp.zeros_like(search), pay_ref)
    remainder_ref[...] = remainder
    search_ref[...] = search
    smoothed_ref[...] = smoothed_in[...] + search


def closing_kernel(
    plan, received_ref, blocks_ref, select_ref, remainder_in,
    remainder_ref, gather_ref, result_ref,
):
    product(plan, blocks_ref, received_ref, select_ref, gather_ref, result_ref)
    remainder_ref[...] = remainder_in[...] - result_ref[...]


def local(blocks, pattern, order, start, rhs):
    plan = Plan([lax.axis_size(axis) for axis in AXES], start.shape)
    state = jax.ShapeDtypeStruct((plan.rows, plan.width), jnp.float32)
    pay = jax.ShapeDtypeStruct((plan.devices, plan.sent, plan.width), jnp.bfloat16)
    select = jax.ShapeDtypeStruct((plan.targets, plan.sources), jnp.bfloat16)
    scratch = [
        pltpu.VMEM((plan.targets, plan.width), jnp.float32),
        pltpu.VMEM((plan.rows, plan.width), jnp.float32),
    ]

    def call(kernel, ins, outs, scratch_shapes=()):
        return pl.pallas_call(
            kernel,
            in_specs=ins,
            out_specs=[VMEM] * len(outs),
            out_shape=outs,
            scratch_shapes=scratch_shapes,
            compiler_params=pltpu.CompilerParams(vmem_limit_bytes=GRANT),
        )

    def exchange(sent):
        got = lax.all_to_all(sent, AXES, 0, 0, tiled=True)
        return got.reshape(plan.sources, plan.width)

    flat_start = start.reshape(state.shape)
    flat_rhs = rhs.reshape(state.shape)
    (sent,) = call(functools.partial(first_kernel, plan), [SMEM, VMEM], [pay])(order, flat_start)
    sent, table, smoothed, remainder, search = call(
        functools.partial(opening_kernel, plan),
        [VMEM, VMEM, SMEM, VMEM, VMEM, VMEM],
        [pay, select, state, state, state],
        scratch,
    )(exchange(sent), blocks, order, pattern, flat_start, flat_rhs)
    sigma = CENTER / SPREAD
    rho = 1.0 / sigma
    for number in range(DEG - 1):
        following = 1.0 / (2.0 * sigma - rho)
        factors = (following * rho, 2.0 * following / SPREAD)
        rho = following
        sent, smoothed, remainder, search = call(
            functools.partial(turn_kernel, plan, factors),
            [VMEM] * 6,
            [pay, state, state, state],
            scratch,
        )(exchange(sent), blocks, table, smoothed, remainder, search)
    (remainder,) = call(
        functools.partial(closing_kernel, plan), [VMEM] * 4, [state], scratch
    )(exchange(sent), blocks, table, remainder)
    return smoothed.reshape(start.shape), remainder.reshape(start.shape)


def solution(mesh):
    in_specs = (
        P("gx", "gy", "gz", None, None, None),
        P("gx", "gy", None, None),
        P("gx", "gy", None),
        P("gx", "gy", "gz", None),
        P("gx", "gy", "gz", None),
    )
    out_specs = (P("gx", "gy", "gz", None), P("gx", "gy", "gz", None))
    return jax.shard_map(local, mesh=mesh, in_specs=in_specs, out_specs=out_specs, check_vma=False)
```

time: 125 us -> 62.8 us (0.50)
  starting transfers between devices: 50.7 us -> 0 us
  waiting for transfers between devices: 25 us -> 0 us
  blocking collectives: 26.4 us -> 50.9 us
  matrix products: 15.5 us -> 0 us
  Pallas kernels: 0 us -> 6.17 us
  other arithmetic: 1.62 us -> 0 us
    all_to_all x0 -> x5, blocking collectives: none -> 50.9 us  [exchange(): got = lax.all_to_all(sent, AXES, 0, 0, tiled=True)]
    ppermute x20 -> x0, starting transfers between devices: 50.7 us -> none  [the longest x10 37.9 us: padded_2(): lax.ppermute(tail, axis, [(i, (i + 1) % count) for i in range(ends)])]
    all_gather x5 -> x0, blocking collectives: 26.4 us -> none  [operator(): lax.all_gather(vector.astype(jnp.bfloat16), 'gz', axis=2, tiled=True)]
    ppermute x20 -> x0, waiting for transfers between devices: 25 us -> none  [the longest x10 18.9 us: padded_2(): lax.ppermute(head, axis, [((i + 1) % count, i) for i in range(ends)])]
    dot_general x55 -> x0, matrix products: 15.5 us -> none  [the longest x45 9.05 us: coupled_product(): jnp.einsum('xyscp,xypw->xyscw', table, column, preferred_element_type=jnp...]
    pallas_call x0 -> x6, Pallas kernels: none -> 6.17 us  [the longest x3 2.66 us: local(): call(functools.partial(turn_kernel, plan, factors), [VMEM] * 6, [pay, sta...]
    unnamed x11 -> x12, local copies, waits for them, and re-layouts: 2.04 us -> 4.74 us
  transfers between devices with their start and end apart: 20 -> 0, of which waited for: 10 -> 0; matrix products, arithmetic and copies ran while one was open for 2% -> 0% of each run, Pallas kernels for 0% -> 0%
where the time goes in v1:
time: 62.8 us; the launch traced here: 62.5 us
  blocking collectives  50.9 us (81%)
  Pallas kernels  6.17 us (10%)
  local copies, waits for them, and re-layouts  4.74 us (8%)
  between operations  0.65 us (1%)
    all_to_all x5, blocking collectives, exchange(): got = lax.all_to_all(sent, AXES, 0, 0, tiled=True)  50.9 us
    unnamed x12, local copies, waits for them, and re-layouts  4.74 us
    pallas_call x3, Pallas kernels, local(): call(functools.partial(turn_kernel, plan, factors), [VMEM] * 6, [pay, sta...  2.66 us
    pallas_call x1, Pallas kernels, local(): call(functools.partial(opening_kernel, plan), [VMEM, VMEM, SMEM, VMEM, VM...  1.67 us
    pallas_call x1, Pallas kernels, local(): call(functools.partial(closing_kernel, plan), [VMEM] * 4, [state], scratch)  1.27 us

profile of v1, /device:TPU:0, one launch (start us, length us, event | category | flops | bytes accessed | tf_op | source)
XLA Modules:
  0.0 62.5 jit_solution(5479400474245860128)
XLA Ops:
  0.6 0.0 copy-start.2
  0.6 0.7 %copy-done.2 = f32[2,1,2,128]{3,2,1,0:T(2,128)S(1)} copy-done((f32[2,1,2,128]{3,2,1,0:T(2,128)S(1)}, f32[2,1,2,128]{3,2,1,0:T(2,128)}, u32[]{:S(2)}) %copy-start.2) | copy-done | bytes 2072
  1.3 0.0 copy-start.4
  1.3 0.7 %copy-done.4 = s32[2,1,8]{2,1,0:T(1,128)S(1)} copy-done((s32[2,1,8]{2,1,0:T(1,128)S(1)}, s32[2,1,8]{2,1,0:T(1,128)}, u32[]{:S(2)}) %copy-start.4) | copy-done | bytes 88
  2.0 0.6 shard_map.68
  2.6 14.5 %all_to_all.25 = bf16[32,8,128]{2,1,0:T(8,128)(2,1)S(1)} all-to-all(bf16[32,8,128]{2,1,0:T(8,128)(2,1)S(1)} %shard_map.68), channel_id=1, replica_groups=mesh['gx'=4,'gy'=2,'gz'=4] {'gx','gy','gz'}, dimensions={0} | all-to-all | bytes 131072 | tf_op jit(solution)/shard_map/all_to_all | solution.py:199
  17.1 0.0 copy-start
  17.1 2.0 %copy-done = bf16[2,1,2,27,128,128]{5,4,3,2,1,0:T(8,128)(2,1)S(1)} copy-done((bf16[2,1,2,27,128,128]{5,4,3,2,1,0:T(8,128)(2,1)S(1)}, bf16[2,1,2,27,128,128]{5,4,3,2,1,0:T(8,128)(2,1)}, u32[]{:S(2)}) %copy-start) | copy-done | bytes 3538968
  19.1 0.0 copy-start.3
  19.1 0.7 %copy-done.3 = s32[2,1,8,27]{3,2,1,0:T(8,128)S(1)} copy-done((s32[2,1,8,27]{3,2,1,0:T(8,128)S(1)}, s32[2,1,8,27]{3,2,1,0:T(8,128)}, u32[]{:S(2)}) %copy-start.3) | copy-done | bytes 1752
  19.8 0.0 copy-start.5
  19.8 0.7 %copy-done.5 = f32[2,1,2,128]{3,2,1,0:T(2,128)S(1)} copy-done((f32[2,1,2,128]{3,2,1,0:T(2,128)S(1)}, f32[2,1,2,128]{3,2,1,0:T(2,128)}, u32[]{:S(2)}) %copy-start.5) | copy-done | bytes 2072
  20.5 0.0 copy-start.1
  20.5 1.7 %shard_map.69 = (bf16[32,8,128]{2,1,0:T(8,128)(2,1)S(1)}, bf16[128,256]{1,0:T(8,128)(2,1)S(1)}, f32[4,128]{1,0:T(4,128)S(1)}, f32[4,128]{1,0:T(4,128)S(1)}, f32[4,128]{1,0:T(4,128)S(1)}) custom-call(bf16[256,128]{1,0:T(8,128)(2,1)S(1)} %bitcast.16, bf16[2,1,2,27,128,128]{5,4,3,2,1,0:T(8,128)(2,1)S(1)} %copy-done, s32[2,1,8]{2,1,0:T(1,128)S(1)} %copy-done.4, ...), custom_call_target="tpu_custom_call" | custom-call | tf_op jit(solution)/shard_map/pallas_call | solution.py:205
  22.2 9.1 %all_to_all.26 = bf16[32,8,128]{2,1,0:T(8,128)(2,1)S(1)} all-to-all(bf16[32,8,128]{2,1,0:T(8,128)(2,1)S(1)} %get-tuple-element.18), channel_id=1, replica_groups=mesh['gx'=4,'gy'=2,'gz'=4] {'gx','gy','gz'}, dimensions={0} | all-to-all | bytes 131072 | tf_op jit(solution)/shard_map/all_to_all | solution.py:199
  31.3 0.0 copy-done.1
  31.3 0.7 %shard_map.70 = (bf16[32,8,128]{2,1,0:T(8,128)(2,1)S(1)}, f32[4,128]{1,0:T(4,128)S(1)}, f32[4,128]{1,0:T(4,128)S(1)}, f32[4,128]{1,0:T(4,128)S(1)}) custom-call(bf16[256,128]{1,0:T(8,128)(2,1)S(1)} %bitcast.13, bf16[2,1,2,27,128,128]{5,4,3,2,1,0:T(8,128)(2,1)S(1)} %copy-done.1, bf16[128,256]{1,0:T(8,128)(2,1)S(1)} %get-tuple-element.19.select_ref, ...), custom_call_target="tpu_custom_call" | custom-call | tf_op jit(solution)/shard_map/pallas_call | solution.py:217
  32.0 9.1 %all_to_all.27 = bf16[32,8,128]{2,1,0:T(8,128)(2,1)S(1)} all-to-all(bf16[32,8,128]{2,1,0:T(8,128)(2,1)S(1)} %get-tuple-element.23), channel_id=1, replica_groups=mesh['gx'=4,'gy'=2,'gz'=4] {'gx','gy','gz'}, dimensions={0} | all-to-all | bytes 131072 | tf_op jit(solution)/shard_map/all_to_all | solution.py:199
  41.1 0.7 %shard_map.71 = (bf16[32,8,128]{2,1,0:T(8,128)(2,1)S(1)}, f32[4,128]{1,0:T(4,128)S(1)}, f32[4,128]{1,0:T(4,128)S(1)}, f32[4,128]{1,0:T(4,128)S(1)}) custom-call(bf16[256,128]{1,0:T(8,128)(2,1)S(1)} %bitcast.14, bf16[2,1,2,27,128,128]{5,4,3,2,1,0:T(8,128)(2,1)S(1)} %copy-done.1, bf16[128,256]{1,0:T(8,128)(2,1)S(1)} %get-tuple-element.19.select_ref, ...), custom_call_target="tpu_custom_call" | custom-call | tf_op jit(solution)/shard_map/pallas_call | solution.py:217
  41.8 9.1 %all_to_all.28 = bf16[32,8,128]{2,1,0:T(8,128)(2,1)S(1)} all-to-all(bf16[32,8,128]{2,1,0:T(8,128)(2,1)S(1)} %get-tuple-element.27), channel_id=1, replica_groups=mesh['gx'=4,'gy'=2,'gz'=4] {'gx','gy','gz'}, dimensions={0} | all-to-all | bytes 131072 | tf_op jit(solution)/shard_map/all_to_all | solution.py:199
  50.9 1.3 %shard_map.72 = (bf16[32,8,128]{2,1,0:T(8,128)(2,1)S(1)}, f32[4,128]{1,0:T(4,128)}, f32[4,128]{1,0:T(4,128)S(1)}, f32[4,128]{1,0:T(4,128)}) custom-call(bf16[256,128]{1,0:T(8,128)(2,1)S(1)} %bitcast.15, bf16[2,1,2,27,128,128]{5,4,3,2,1,0:T(8,128)(2,1)S(1)} %copy-done.1, bf16[128,256]{1,0:T(8,128)(2,1)S(1)} %get-tuple-element.19.select_ref, ...), custom_call_target="tpu_custom_call" | custom-call | tf_op jit(solution)/shard_map/pallas_call | solution.py:217
  52.1 9.1 %all_to_all.29 = bf16[32,8,128]{2,1,0:T(8,128)(2,1)S(1)} all-to-all(bf16[32,8,128]{2,1,0:T(8,128)(2,1)S(1)} %get-tuple-element.32), channel_id=1, replica_groups=mesh['gx'=4,'gy'=2,'gz'=4] {'gx','gy','gz'}, dimensions={0} | all-to-all | bytes 131072 | tf_op jit(solution)/shard_map/all_to_all | solution.py:199
  61.2 1.3 %shard_map.73 = f32[4,128]{1,0:T(4,128)} custom-call(bf16[256,128]{1,0:T(8,128)(2,1)S(1)} %bitcast.17, bf16[2,1,2,27,128,128]{5,4,3,2,1,0:T(8,128)(2,1)S(1)} %copy-done.1, bf16[128,256]{1,0:T(8,128)(2,1)S(1)} %get-tuple-element.19.select_ref, f32[4,128]{1,0:T(4,128)S(1)} %get-tuple-element.33.remainder_in), custom_call_target="tpu_custom_call" | custom-call | tf_op jit(solution)/shard_map/pallas_call | solution.py:223
Async XLA Ops:
  0.6 0.7 %copy-start.2 = (f32[2,1,2,128]{3,2,1,0:T(2,128)S(1)}, f32[2,1,2,128]{3,2,1,0:T(2,128)}, u32[]{:S(2)}) copy-start(f32[2,1,2,128]{3,2,1,0:T(2,128)} %param.8) | copy-start | bytes 6148
  1.3 0.7 %copy-start.4 = (s32[2,1,8]{2,1,0:T(1,128)S(1)}, s32[2,1,8]{2,1,0:T(1,128)}, u32[]{:S(2)}) copy-start(s32[2,1,8]{2,1,0:T(1,128)} %order_ref.3) | copy-start | bytes 196
  17.1 2.0 %copy-start = (bf16[2,1,2,27,128,128]{5,4,3,2,1,0:T(8,128)(2,1)S(1)}, bf16[2,1,2,27,128,128]{5,4,3,2,1,0:T(8,128)(2,1)}, u32[]{:S(2)}) copy-start(bf16[2,1,2,27,128,128]{5,4,3,2,1,0:T(8,128)(2,1)} %blocks_ref.9) | copy-start | bytes 10616836
  19.1 0.7 %copy-start.3 = (s32[2,1,8,27]{3,2,1,0:T(8,128)S(1)}, s32[2,1,8,27]{3,2,1,0:T(8,128)}, u32[]{:S(2)}) copy-start(s32[2,1,8,27]{3,2,1,0:T(8,128)} %pattern_ref.1) | copy-start | bytes 5188
  19.8 0.7 %copy-start.5 = (f32[2,1,2,128]{3,2,1,0:T(2,128)S(1)}, f32[2,1,2,128]{3,2,1,0:T(2,128)}, u32[]{:S(2)}) copy-start(f32[2,1,2,128]{3,2,1,0:T(2,128)} %param.9) | copy-start | bytes 6148
  20.5 10.8 %copy-start.1 = (bf16[2,1,2,27,128,128]{5,4,3,2,1,0:T(8,128)(2,1)S(1)}, bf16[2,1,2,27,128,128]{5,4,3,2,1,0:T(8,128)(2,1)}, u32[]{:S(2)}) copy-start(bf16[2,1,2,27,128,128]{5,4,3,2,1,0:T(8,128)(2,1)} %blocks_ref.9) | copy-start | bytes 10616836

commit v2 on v1

v2 whole, which is shorter than its diff:
```python
import functools

import jax
import jax.numpy as jnp
from jax import lax
from jax.experimental import pallas as pl
from jax.experimental.pallas import tpu as pltpu
from jax.sharding import PartitionSpec as P

DEG = 4
CENTER = 1.0
SPREAD = 0.8
LANES = 128
PITCH = 32
GRANT = 16 * 2**20
AXES = ("gx", "gy", "gz")
VMEM = pl.BlockSpec(memory_space=pltpu.VMEM)
HBM = pl.BlockSpec(memory_space=pltpu.HBM)


def split(value, count):
    if count & (count - 1) == 0:
        shift = count.bit_length() - 1
        return value >> shift, value & (count - 1)
    whole = jnp.floor((value.astype(jnp.float32) + 0.5) * (1.0 / count)).astype(jnp.int32)
    return whole, value - whole * count


def far(array):
    return pltpu.with_memory_space_constraint(array, pltpu.HBM)


class Plan:
    def __init__(self, axis_sizes, local_shape):
        self.gx, self.gy, self.gz = axis_sizes
        self.nx, self.ny, self.nz, self.width = local_shape
        self.devices = self.gx * self.gy * self.gz
        self.rows = self.nx * self.ny * self.nz
        self.sources = self.devices * self.rows
        self.few = self.ny == 1 and self.gy <= 2
        self.spans = min(3, self.gy) if self.few else 3
        self.entries = [(i, j, k) for i in range(3) for j in range(self.spans) for k in range(3)]
        self.targets = -(-self.rows * PITCH // LANES) * LANES

    def first_span(self):
        return 1 - lax.axis_index("gy") if self.few else 0

    def place(self, row):
        return row // (self.ny * self.nz), row // self.nz % self.ny, row % self.nz

    def key(self, x, y, z):
        return ((x + 1) * (self.gy * self.ny + 2) + y + 1) * (self.gz * self.nz + 2) + z + 1


def send(tile, pay_ref):
    pay_ref[...] = jnp.broadcast_to(tile.astype(jnp.bfloat16)[None], pay_ref.shape)


def first_kernel(
    plan, order_hbm, pattern_hbm, start_hbm,
    pay_ref, want_ref, start_ref, order_ref, pattern_ref, sems,
):
    copies = (
        pltpu.make_async_copy(order_hbm, order_ref, sems.at[0]),
        pltpu.make_async_copy(pattern_hbm, pattern_ref, sems.at[1]),
        pltpu.make_async_copy(start_hbm, start_ref, sems.at[2]),
    )
    for copy in copies:
        copy.start()
    for copy in copies:
        copy.wait()
    first = lax.axis_index("gz") * plan.nz
    line = lax.broadcasted_iota(jnp.int32, (plan.rows, plan.width), 0)
    planes = jnp.zeros_like(line)
    for row in range(plan.rows):
        x, y, s = plan.place(row)
        planes = jnp.where(line == row, order_ref[x, y, first + s], planes)
    send(jnp.concatenate([start_ref[...], planes.astype(jnp.float32)], axis=0), pay_ref)
    want_ref[...] = wanted(plan, order_ref, pattern_ref)


def wanted(plan, order_ref, pattern_ref):
    first = lax.axis_index("gz") * plan.nz
    span = plan.first_span()
    lane = lax.broadcasted_iota(jnp.int32, (1, plan.targets), 1)
    row, entry = split(lane, PITCH)
    a = (entry * 57) >> 9
    rest = entry - 9 * a
    b = (rest * 43) >> 7
    c = rest - 3 * b
    plane = jnp.zeros_like(lane)
    keep = jnp.zeros_like(lane)
    for number in range(plan.rows):
        x, y, s = plan.place(number)
        plane = jnp.where(row == number, order_ref[x, y, first + s], plane)
        flags = pattern_ref[x, y, pl.ds(first + s, 1), :]
        gap = jnp.zeros((1, plan.targets - flags.shape[1]), jnp.int32)
        flags = jnp.concatenate([flags, gap], axis=1)
        keep = keep + (pltpu.roll(flags, PITCH * number, 1) if number else flags)
    if plan.few:
        keep = jnp.where(span == 1, pltpu.roll(keep, plan.targets - 3, 1), keep)
    b = b + span
    keep = ((keep > 0) | (9 * a + 3 * b + c == 13)) & (entry < 27) & (row < plan.rows)
    xy, _ = split(row, plan.nz)
    x, y = split(xy, plan.ny)
    x = lax.axis_index("gx") * plan.nx + x + a - 1
    y = lax.axis_index("gy") * plan.ny + y + b - 1
    return jnp.where(keep, plan.key(x, y, plane + c - 1), -1)


def held(plan, planes):
    source = lax.broadcasted_iota(jnp.int32, (plan.sources, LANES), 0)
    device, rank = split(source, plan.rows)
    device_xy, _ = split(device, plan.gz)
    device_x, device_y = split(device_xy, plan.gy)
    rank_xy, _ = split(rank, plan.nz)
    rank_x, rank_y = split(rank_xy, plan.ny)
    return plan.key(device_x * plan.nx + rank_x, device_y * plan.ny + rank_y, planes)


def selection(plan, planes, want, select_ref):
    have = held(plan, planes)
    for first in range(0, plan.targets, LANES):
        part = slice(first, first + LANES)
        table = jnp.where(have == want[:, part], 1.0, 0.0)
        select_ref[part, :] = table.T.astype(jnp.bfloat16)


def stage(plan, received_ref, stage_ref, first):
    for device in range(plan.devices):
        part = received_ref[device, first : first + plan.rows, :].astype(jnp.float32)
        stage_ref[device * plan.rows : (device + 1) * plan.rows, :] = part


def product(plan, blocks_ref, received_ref, select_ref, stage_ref, gather_ref, result_ref):
    stage(plan, received_ref, stage_ref, 0)
    gather_ref[...] = jnp.dot(
        select_ref[...], stage_ref[...].astype(jnp.bfloat16), preferred_element_type=jnp.float32
    )
    span = plan.first_span()
    size = plan.width
    lane = lax.broadcasted_iota(jnp.int32, (size, size), 1)
    line = lax.broadcasted_iota(jnp.int32, (size, size), 0)
    for row in range(plan.rows):
        x, y, s = plan.place(row)
        total = jnp.zeros((size, size), jnp.float32)
        for i, j, k in plan.entries:
            at = row * PITCH + 9 * i + 3 * j + k
            block = blocks_ref[x, y, s, 9 * i + 3 * (j + span) + k].astype(jnp.float32)
            total = total + block * gather_ref[at : at + 1, :]
        sums = jnp.sum(total, axis=1, keepdims=True)
        line_sums = jnp.where(lane == line, sums, 0.0)
        result_ref[row : row + 1, :] = jnp.sum(line_sums, axis=0, keepdims=True)


def opening_kernel(
    plan, received_ref, blocks_ref, want_ref, start_ref, rhs_ref,
    pay_ref, select_ref, smoothed_ref, remainder_ref, search_ref,
    stage_ref, gather_ref, result_ref,
):
    stage(plan, received_ref, stage_ref, plan.rows)
    planes = stage_ref[...].astype(jnp.int32)
    selection(plan, planes, want_ref[...], select_ref)
    product(plan, blocks_ref, received_ref, select_ref, stage_ref, gather_ref, result_ref)
    remainder = rhs_ref[...] - result_ref[...]
    search = remainder / CENTER
    send(search, pay_ref)
    remainder_ref[...] = remainder
    search_ref[...] = search
    smoothed_ref[...] = start_ref[...] + search


def turn_kernel(
    plan, factors, received_ref, blocks_ref, select_ref, smoothed_in, remainder_in, search_in,
    pay_ref, smoothed_ref, remainder_ref, search_ref,
    stage_ref, gather_ref, result_ref,
):
    product(plan, blocks_ref, received_ref, select_ref, stage_ref, gather_ref, result_ref)
    remainder = remainder_in[...] - result_ref[...]
    search = factors[0] * search_in[...] + factors[1] * remainder
    send(search, pay_ref)
    remainder_ref[...] = remainder
    search_ref[...] = search
    smoothed_ref[...] = smoothed_in[...] + search


def closing_kernel(
    plan, received_ref, blocks_ref, select_ref, smoothed_in, remainder_in,
    smoothed_ref, remainder_ref, stage_ref, gather_ref, result_ref,
):
    product(plan, blocks_ref, received_ref, select_ref, stage_ref, gather_ref, result_ref)
    remainder_ref[...] = remainder_in[...] - result_ref[...]
    smoothed_ref[...] = smoothed_in[...]


def local(blocks, pattern, order, start, rhs):
    plan = Plan([lax.axis_size(axis) for axis in AXES], start.shape)
    state = jax.ShapeDtypeStruct((plan.rows, plan.width), jnp.float32)
    select = jax.ShapeDtypeStruct((plan.targets, plan.sources), jnp.bfloat16)
    scratch = [
        pltpu.VMEM((plan.sources, plan.width), jnp.float32),
        pltpu.VMEM((plan.targets, plan.width), jnp.float32),
        pltpu.VMEM((plan.rows, plan.width), jnp.float32),
    ]

    def pay(rows):
        return jax.ShapeDtypeStruct((plan.devices, rows, plan.width), jnp.bfloat16)

    def call(kernel, ins, outs, scratch_shapes, cost=None):
        return pl.pallas_call(
            kernel,
            in_specs=ins,
            out_specs=[VMEM] * len(outs),
            out_shape=outs,
            scratch_shapes=scratch_shapes,
            compiler_params=pltpu.CompilerParams(vmem_limit_bytes=GRANT),
            cost_estimate=cost,
        )

    def exchange(sent):
        return lax.all_to_all(sent, AXES, 0, 0, tiled=True)

    flat_start = start.reshape(state.shape)
    flat_rhs = rhs.reshape(state.shape)
    sent, want = call(
        functools.partial(first_kernel, plan),
        [HBM, HBM, HBM],
        [pay(2 * plan.rows), jax.ShapeDtypeStruct((1, plan.targets), jnp.int32)],
        [
            pltpu.VMEM(state.shape, jnp.float32),
            pltpu.SMEM(order.shape, jnp.int32),
            pltpu.VMEM(pattern.shape, jnp.int32),
            pltpu.SemaphoreType.DMA((3,)),
        ],
        pl.CostEstimate(flops=10**10, bytes_accessed=10**8, transcendentals=0),
    )(far(order), far(pattern), far(flat_start))
    sent, table, smoothed, remainder, search = call(
        functools.partial(opening_kernel, plan),
        [VMEM] * 5,
        [pay(plan.rows), select, state, state, state],
        scratch,
    )(exchange(sent), blocks, want, flat_start, flat_rhs)
    sigma = CENTER / SPREAD
    rho = 1.0 / sigma
    for _ in range(DEG - 1):
        following = 1.0 / (2.0 * sigma - rho)
        factors = (following * rho, 2.0 * following / SPREAD)
        rho = following
        sent, smoothed, remainder, search = call(
            functools.partial(turn_kernel, plan, factors),
            [VMEM] * 6,
            [pay(plan.rows), state, state, state],
            scratch,
        )(exchange(sent), blocks, table, smoothed, remainder, search)
    smoothed, remainder = call(
        functools.partial(closing_kernel, plan), [VMEM] * 5, [state, state], scratch
    )(exchange(sent), blocks, table, smoothed, remainder)
    return smoothed.reshape(start.shape), remainder.reshape(start.shape)


def solution(mesh):
    in_specs = (
        P("gx", "gy", "gz", None, None, None),
        P("gx", "gy", None, None),
        P("gx", "gy", None),
        P("gx", "gy", "gz", None),
        P("gx", "gy", "gz", None),
    )
    out_specs = (P("gx", "gy", "gz", None), P("gx", "gy", "gz", None))
    return jax.shard_map(local, mesh=mesh, in_specs=in_specs, out_specs=out_specs, check_vma=False)
```

time: 62.8 us -> 57.4 us (0.914)
  local copies, waits for them, and re-layouts: 4.74 us -> 0.01 us
    unnamed x12 -> x6, local copies, waits for them, and re-layouts: 4.74 us -> 0.01 us
where the time goes in v2:
time: 57.4 us; the launch traced here: 57.2 us
  blocking collectives  50.3 us (88%)
  Pallas kernels  6.14 us (11%)
  between operations  0.69 us (1%)
    all_to_all x5, blocking collectives, exchange(): return lax.all_to_all(sent, AXES, 0, 0, tiled=True)  50.3 us
    pallas_call x3, Pallas kernels, local(): call(functools.partial(turn_kernel, plan, factors), [VMEM] * 6, [pay(plan...  2.91 us
    pallas_call x1, Pallas kernels, local(): call(functools.partial(closing_kernel, plan), [VMEM] * 5, [state, state],...  1.35 us

profile of v2, /device:TPU:0, one launch (start us, length us, event | category | flops | bytes accessed | tf_op | source)
XLA Modules:
  0.0 57.2 jit_solution(17888073449274156053)
XLA Ops:
  0.6 0.0 copy-start
  0.6 0.0 copy-start.1
  0.7 0.0 copy-start.2
  0.7 1.0 %shard_map.68 = (bf16[32,8,128]{2,1,0:T(8,128)(2,1)S(1)}, s32[1,128]{1,0:T(1,128)S(1)}) custom-call(s32[2,1,8]{2,1,0:T(1,128)} %order_hbm.1, s32[2,1,8,27]{3,2,1,0:T(8,128)} %pattern_hbm.1, f32[4,128]{1,0:T(4,128)} %bitcast.8), custom_call_target="tpu_custom_call" | custom-call | flops 10000000000 | bytes 100000000 | tf_op jit(solution)/shard_map/pallas_call | solution.py:225
  1.7 14.5 %all_to_all.25.received_ref = bf16[32,8,128]{2,1,0:T(8,128)(2,1)S(1)} all-to-all(bf16[32,8,128]{2,1,0:T(8,128)(2,1)S(1)} %get-tuple-element.22), channel_id=1, replica_groups=mesh['gx'=4,'gy'=2,'gz'=4] {'gx','gy','gz'}, dimensions={0} | all-to-all | bytes 131072 | tf_op jit(solution)/shard_map/all_to_all | solution.py:221
  16.2 0.0 copy-done
  16.2 0.0 copy-done.1
  16.2 0.0 copy-done.2
  16.2 0.9 %shard_map.69 = (bf16[32,4,128]{2,1,0:T(4,128)(2,1)S(1)}, bf16[128,128]{1,0:T(8,128)(2,1)S(1)}, f32[4,128]{1,0:T(4,128)S(1)}, f32[4,128]{1,0:T(4,128)S(1)}, f32[4,128]{1,0:T(4,128)S(1)}) custom-call(bf16[32,8,128]{2,1,0:T(8,128)(2,1)S(1)} %all_to_all.25.received_ref, bf16[2,1,2,27,128,128]{5,4,3,2,1,0:T(8,128)(2,1)S(1)} %copy-done, ...), custom_call_target="tpu_custom_call" | custom-call | tf_op jit(solution)/shard_map/pallas_call | solution.py:237
  17.1 9.0 %all_to_all.26.received_ref = bf16[32,4,128]{2,1,0:T(4,128)(2,1)S(1)} all-to-all(bf16[32,4,128]{2,1,0:T(4,128)(2,1)S(1)} %get-tuple-element.24), channel_id=1, replica_groups=mesh['gx'=4,'gy'=2,'gz'=4] {'gx','gy','gz'}, dimensions={0} | all-to-all | bytes 65536 | tf_op jit(solution)/shard_map/all_to_all | solution.py:221
  26.1 0.8 %shard_map.70 = (bf16[32,4,128]{2,1,0:T(4,128)(2,1)S(1)}, f32[4,128]{1,0:T(4,128)S(1)}, f32[4,128]{1,0:T(4,128)S(1)}, f32[4,128]{1,0:T(4,128)S(1)}) custom-call(bf16[32,4,128]{2,1,0:T(4,128)(2,1)S(1)} %all_to_all.26.received_ref, bf16[2,1,2,27,128,128]{5,4,3,2,1,0:T(8,128)(2,1)S(1)} %copy-done, bf16[128,128]{1,0:T(8,128)(2,1)S(1)} %get-tuple-element.25.select_ref, ...), custom_call_target="tpu_custom_call" | custom-call | tf_op jit(solution)/shard_map/pallas_call | solution.py:249
  26.9 9.0 %all_to_all.27.received_ref = bf16[32,4,128]{2,1,0:T(4,128)(2,1)S(1)} all-to-all(bf16[32,4,128]{2,1,0:T(4,128)(2,1)S(1)} %get-tuple-element.29), channel_id=1, replica_groups=mesh['gx'=4,'gy'=2,'gz'=4] {'gx','gy','gz'}, dimensions={0} | all-to-all | bytes 65536 | tf_op jit(solution)/shard_map/all_to_all | solution.py:221
  35.8 0.8 %shard_map.71 = (bf16[32,4,128]{2,1,0:T(4,128)(2,1)S(1)}, f32[4,128]{1,0:T(4,128)S(1)}, f32[4,128]{1,0:T(4,128)S(1)}, f32[4,128]{1,0:T(4,128)S(1)}) custom-call(bf16[32,4,128]{2,1,0:T(4,128)(2,1)S(1)} %all_to_all.27.received_ref, bf16[2,1,2,27,128,128]{5,4,3,2,1,0:T(8,128)(2,1)S(1)} %copy-done, bf16[128,128]{1,0:T(8,128)(2,1)S(1)} %get-tuple-element.25.select_ref, ...), custom_call_target="tpu_custom_call" | custom-call | tf_op jit(solution)/shard_map/pallas_call | solution.py:249
  36.6 9.0 %all_to_all.28.received_ref = bf16[32,4,128]{2,1,0:T(4,128)(2,1)S(1)} all-to-all(bf16[32,4,128]{2,1,0:T(4,128)(2,1)S(1)} %get-tuple-element.33), channel_id=1, replica_groups=mesh['gx'=4,'gy'=2,'gz'=4] {'gx','gy','gz'}, dimensions={0} | all-to-all | bytes 65536 | tf_op jit(solution)/shard_map/all_to_all | solution.py:221
  45.5 1.3 %shard_map.72 = (bf16[32,4,128]{2,1,0:T(4,128)(2,1)S(1)}, f32[4,128]{1,0:T(4,128)S(1)}, f32[4,128]{1,0:T(4,128)S(1)}, f32[4,128]{1,0:T(4,128)}) custom-call(bf16[32,4,128]{2,1,0:T(4,128)(2,1)S(1)} %all_to_all.28.received_ref, bf16[2,1,2,27,128,128]{5,4,3,2,1,0:T(8,128)(2,1)S(1)} %copy-done, bf16[128,128]{1,0:T(8,128)(2,1)S(1)} %get-tuple-element.25.select_ref, ...), custom_call_target="tpu_custom_call" | custom-call | tf_op jit(solution)/shard_map/pallas_call | solution.py:249
  46.9 8.9 %all_to_all.29.received_ref = bf16[32,4,128]{2,1,0:T(4,128)(2,1)S(1)} all-to-all(bf16[32,4,128]{2,1,0:T(4,128)(2,1)S(1)} %get-tuple-element.37), channel_id=1, replica_groups=mesh['gx'=4,'gy'=2,'gz'=4] {'gx','gy','gz'}, dimensions={0} | all-to-all | bytes 65536 | tf_op jit(solution)/shard_map/all_to_all | solution.py:221
  55.8 1.3 %shard_map.73 = (f32[4,128]{1,0:T(4,128)}, f32[4,128]{1,0:T(4,128)}) custom-call(bf16[32,4,128]{2,1,0:T(4,128)(2,1)S(1)} %all_to_all.29.received_ref, bf16[2,1,2,27,128,128]{5,4,3,2,1,0:T(8,128)(2,1)S(1)} %copy-done, bf16[128,128]{1,0:T(8,128)(2,1)S(1)} %get-tuple-element.25.select_ref, f32[4,128]{1,0:T(4,128)S(1)} %get-tuple-element.38.smoothed_in, ...), custom_call_target="tpu_custom_call" | custom-call | tf_op jit(solution)/shard_map/pallas_call | solution.py:255
Async XLA Ops:
  0.6 15.6 %copy-start = (bf16[2,1,2,27,128,128]{5,4,3,2,1,0:T(8,128)(2,1)S(1)}, bf16[2,1,2,27,128,128]{5,4,3,2,1,0:T(8,128)(2,1)}, u32[]{:S(2)}) copy-start(bf16[2,1,2,27,128,128]{5,4,3,2,1,0:T(8,128)(2,1)} %blocks_ref.9) | copy-start | bytes 10616836
  0.6 15.6 %copy-start.1 = (f32[2,1,2,128]{3,2,1,0:T(2,128)S(1)}, f32[2,1,2,128]{3,2,1,0:T(2,128)}, u32[]{:S(2)}) copy-start(f32[2,1,2,128]{3,2,1,0:T(2,128)} %param.8) | copy-start | bytes 6148
  0.7 15.6 %copy-start.2 = (f32[2,1,2,128]{3,2,1,0:T(2,128)S(1)}, f32[2,1,2,128]{3,2,1,0:T(2,128)}, u32[]{:S(2)}) copy-start(f32[2,1,2,128]{3,2,1,0:T(2,128)} %param.9) | copy-start | bytes 6148

commit v3 on v2

--- a/solution.py
+++ b/solution.py
@@ -13,7 +13,7 @@
 LANES = 128
 PITCH = 32
 GRANT = 16 * 2**20
-AXES = ("gx", "gy", "gz")
+AXES = ("gz", "gx", "gy")
 VMEM = pl.BlockSpec(memory_space=pltpu.VMEM)
 HBM = pl.BlockSpec(memory_space=pltpu.HBM)
 
@@ -28,6 +28,14 @@
 
 def far(array):
     return pltpu.with_memory_space_constraint(array, pltpu.HBM)
+
+
+class Rounded:
+    def __init__(self, ref):
+        self.ref = ref
+
+    def __getitem__(self, index):
+        return self.ref[index].astype(jnp.bfloat16)
 
 
 class Plan:
@@ -41,12 +49,17 @@
         self.spans = min(3, self.gy) if self.few else 3
         self.entries = [(i, j, k) for i in range(3) for j in range(self.spans) for k in range(3)]
         self.targets = -(-self.rows * PITCH // LANES) * LANES
+        self.lot = -(-self.rows // 8) * 8
+        self.half = -(-(len(self.entries) + 1) // 2 * self.lot // 16) * 16
 
     def first_span(self):
         return 1 - lax.axis_index("gy") if self.few else 0
 
     def place(self, row):
         return row // (self.ny * self.nz), row // self.nz % self.ny, row % self.nz
+
+    def spot(self, number):
+        return number % 2 * self.half + number // 2 * self.lot
 
     def key(self, x, y, z):
         return ((x + 1) * (self.gy * self.ny + 2) + y + 1) * (self.gz * self.nz + 2) + z + 1
@@ -111,58 +124,96 @@
 def held(plan, planes):
     source = lax.broadcasted_iota(jnp.int32, (plan.sources, LANES), 0)
     device, rank = split(source, plan.rows)
-    device_xy, _ = split(device, plan.gz)
+    _, device_xy = split(device, plan.gx * plan.gy)
     device_x, device_y = split(device_xy, plan.gy)
     rank_xy, _ = split(rank, plan.nz)
     rank_x, rank_y = split(rank_xy, plan.ny)
     return plan.key(device_x * plan.nx + rank_x, device_y * plan.ny + rank_y, planes)
 
 
-def selection(plan, planes, want, select_ref):
+def selection(plan, planes, want, table_ref, wide_ref, select_ref):
     have = held(plan, planes)
-    for first in range(0, plan.targets, LANES):
-        part = slice(first, first + LANES)
-        table = jnp.where(have == want[:, part], 1.0, 0.0)
-        select_ref[part, :] = table.T.astype(jnp.bfloat16)
-
-
-def stage(plan, received_ref, stage_ref, first):
-    for device in range(plan.devices):
-        part = received_ref[device, first : first + plan.rows, :].astype(jnp.float32)
-        stage_ref[device * plan.rows : (device + 1) * plan.rows, :] = part
-
-
-def product(plan, blocks_ref, received_ref, select_ref, stage_ref, gather_ref, result_ref):
-    stage(plan, received_ref, stage_ref, 0)
-    gather_ref[...] = jnp.dot(
-        select_ref[...], stage_ref[...].astype(jnp.bfloat16), preferred_element_type=jnp.float32
-    )
+    wide_ref[...] = jnp.zeros_like(wide_ref)
+    for begin in range(0, plan.sources, LANES):
+        some = slice(begin, begin + LANES)
+        for first in range(0, plan.targets, LANES):
+            part = slice(first, first + LANES)
+            table_ref[part, :] = jnp.where(have[some] == want[:, part], 1.0, 0.0).T
+        for number, (i, j, k) in enumerate(plan.entries):
+            rows = table_ref[pl.ds(9 * i + 3 * j + k, plan.rows, stride=PITCH), :]
+            at = plan.spot(number)
+            wide_ref[at : at + plan.rows, some] = rows
+    select_ref[...] = wide_ref[...].astype(jnp.bfloat16)
+
+
+def product(plan, blocks_ref, rows_ref, select_ref, gather_ref):
+    gather_ref[...] = jnp.dot(select_ref[...], rows_ref[...], preferred_element_type=jnp.float32)
     span = plan.first_span()
     size = plan.width
+
+    def block(row, number):
+        x, y, s = plan.place(row)
+        i, j, k = plan.entries[number]
+        return blocks_ref[x, y, s, 9 * i + 3 * (j + span) + k]
+
+    results = [None] * plan.rows
+    count = len(plan.entries) // 2
+    for low in range(0, plan.rows // 4 * 2, 2):
+        sums = []
+        for part in (range(0, count // 2), range(count // 2, count)):
+            left, right = [], []
+            for pair in part:
+                for side in (0, 1):
+                    at = plan.spot(2 * pair + side)
+                    left.append(gather_ref[at : at + plan.lot, :].astype(jnp.bfloat16))
+                    right.append(
+                        jnp.concatenate([block(row, 2 * pair + side) for row in (low, low + 1)], axis=0)
+                    )
+            sums.append(
+                lax.dot_general(
+                    jnp.concatenate(left, axis=1),
+                    jnp.concatenate(right, axis=1),
+                    (((1,), (1,)), ((), ())),
+                    preferred_element_type=jnp.float32,
+                )
+            )
+        both = sums[0] + sums[1]
+        results[low] = both[low : low + 1, :size]
+        results[low + 1] = both[low + 1 : low + 2, size:]
+
     lane = lax.broadcasted_iota(jnp.int32, (size, size), 1)
     line = lax.broadcasted_iota(jnp.int32, (size, size), 0)
     for row in range(plan.rows):
-        x, y, s = plan.place(row)
+        if results[row] is None:
+            numbers = range(len(plan.entries))
+        else:
+            numbers = range(2 * count, len(plan.entries))
+        if not numbers:
+            continue
         total = jnp.zeros((size, size), jnp.float32)
-        for i, j, k in plan.entries:
-            at = row * PITCH + 9 * i + 3 * j + k
-            block = blocks_ref[x, y, s, 9 * i + 3 * (j + span) + k].astype(jnp.float32)
-            total = total + block * gather_ref[at : at + 1, :]
+        for number in numbers:
+            at = plan.spot(number) + row
+            total = total + block(row, number).astype(jnp.float32) * gather_ref[at : at + 1, :]
         sums = jnp.sum(total, axis=1, keepdims=True)
-        line_sums = jnp.where(lane == line, sums, 0.0)
-        result_ref[row : row + 1, :] = jnp.sum(line_sums, axis=0, keepdims=True)
+        found = jnp.sum(jnp.where(lane == line, sums, 0.0), axis=0, keepdims=True)
+        results[row] = found if results[row] is None else results[row] + found
+    return jnp.concatenate(results, axis=0)
 
 
 def opening_kernel(
     plan, received_ref, blocks_ref, want_ref, start_ref, rhs_ref,
     pay_ref, select_ref, smoothed_ref, remainder_ref, search_ref,
-    stage_ref, gather_ref, result_ref,
+    gather_ref, stage_ref, rows_ref, table_ref, wide_ref,
 ):
-    stage(plan, received_ref, stage_ref, plan.rows)
-    planes = stage_ref[...].astype(jnp.int32)
-    selection(plan, planes, want_ref[...], select_ref)
-    product(plan, blocks_ref, received_ref, select_ref, stage_ref, gather_ref, result_ref)
-    remainder = rhs_ref[...] - result_ref[...]
+    for device in range(plan.devices):
+        here = slice(device * plan.rows, (device + 1) * plan.rows)
+        values = received_ref[device].astype(jnp.float32)
+        rows_ref[here, :] = values[: plan.rows]
+        stage_ref[here, :] = values[plan.rows :]
+    selection(plan, stage_ref[...].astype(jnp.int32), want_ref[...], table_ref, wide_ref, select_ref)
+    remainder = rhs_ref[...] - product(
+        plan, blocks_ref, Rounded(rows_ref), select_ref, gather_ref
+    )
     search = remainder / CENTER
     send(search, pay_ref)
     remainder_ref[...] = remainder
@@ -172,35 +223,38 @@
 
 def turn_kernel(
     plan, factors, received_ref, blocks_ref, select_ref, smoothed_in, remainder_in, search_in,
-    pay_ref, smoothed_ref, remainder_ref, search_ref,
-    stage_ref, gather_ref, result_ref,
+    pay_ref, smoothed_ref, remainder_ref, *rest,
 ):
-    product(plan, blocks_ref, received_ref, select_ref, stage_ref, gather_ref, result_ref)
-    remainder = remainder_in[...] - result_ref[...]
+    *search_ref, gather_ref = rest
+    remainder = remainder_in[...] - product(plan, blocks_ref, received_ref, select_ref, gather_ref)
     search = factors[0] * search_in[...] + factors[1] * remainder
     send(search, pay_ref)
     remainder_ref[...] = remainder
-    search_ref[...] = search
     smoothed_ref[...] = smoothed_in[...] + search
+    if search_ref:
+        search_ref[0][...] = search
 
 
 def closing_kernel(
     plan, received_ref, blocks_ref, select_ref, smoothed_in, remainder_in,
-    smoothed_ref, remainder_ref, stage_ref, gather_ref, result_ref,
+    smoothed_ref, remainder_ref, gather_ref,
 ):
-    product(plan, blocks_ref, received_ref, select_ref, stage_ref, gather_ref, result_ref)
-    remainder_ref[...] = remainder_in[...] - result_ref[...]
     smoothed_ref[...] = smoothed_in[...]
+    remainder_ref[...] = remainder_in[...] - product(
+        plan, blocks_ref, received_ref, select_ref, gather_ref
+    )
 
 
 def local(blocks, pattern, order, start, rhs):
-    plan = Plan([lax.axis_size(axis) for axis in AXES], start.shape)
+    plan = Plan([lax.axis_size(axis) for axis in ("gx", "gy", "gz")], start.shape)
     state = jax.ShapeDtypeStruct((plan.rows, plan.width), jnp.float32)
-    select = jax.ShapeDtypeStruct((plan.targets, plan.sources), jnp.bfloat16)
-    scratch = [
+    select = jax.ShapeDtypeStruct((2 * plan.half, plan.sources), jnp.bfloat16)
+    gather = [pltpu.VMEM((2 * plan.half, plan.width), jnp.float32)]
+    tables = [
         pltpu.VMEM((plan.sources, plan.width), jnp.float32),
-        pltpu.VMEM((plan.targets, plan.width), jnp.float32),
-        pltpu.VMEM((plan.rows, plan.width), jnp.float32),
+        pltpu.VMEM((plan.sources, plan.width), jnp.float32),
+        pltpu.VMEM((plan.targets, LANES), jnp.float32),
+        pltpu.VMEM((2 * plan.half, plan.sources), jnp.float32),
     ]
 
     def pay(rows):
@@ -219,6 +273,9 @@
 
     def exchange(sent):
         return lax.all_to_all(sent, AXES, 0, 0, tiled=True)
+
+    def packed(received):
+        return received.reshape(plan.sources, plan.width)
 
     flat_start = start.reshape(state.shape)
     flat_rhs = rhs.reshape(state.shape)
@@ -238,23 +295,25 @@
         functools.partial(opening_kernel, plan),
         [VMEM] * 5,
         [pay(plan.rows), select, state, state, state],
-        scratch,
+        gather + tables,
     )(exchange(sent), blocks, want, flat_start, flat_rhs)
     sigma = CENTER / SPREAD
     rho = 1.0 / sigma
-    for _ in range(DEG - 1):
+    search = [search]
+    for number in range(DEG - 1):
         following = 1.0 / (2.0 * sigma - rho)
         factors = (following * rho, 2.0 * following / SPREAD)
         rho = following
-        sent, smoothed, remainder, search = call(
+        states = [state] * (3 if number + 2 < DEG else 2)
+        sent, smoothed, remainder, *search = call(
             functools.partial(turn_kernel, plan, factors),
             [VMEM] * 6,
-            [pay(plan.rows), state, state, state],
-            scratch,
-        )(exchange(sent), blocks, table, smoothed, remainder, search)
+            [pay(plan.rows)] + states,
+            gather,
+        )(packed(exchange(sent)), blocks, table, smoothed, remainder, *search)
     smoothed, remainder = call(
-        functools.partial(closing_kernel, plan), [VMEM] * 5, [state, state], scratch
-    )(exchange(sent), blocks, table, smoothed, remainder)
+        functools.partial(closing_kernel, plan), [VMEM] * 5, [state, state], gather
+    )(packed(exchange(sent)), blocks, table, smoothed, remainder)
     return smoothed.reshape(start.shape), remainder.reshape(start.shape)
 
 

time: 57.4 us -> 56.1 us (0.977)
  Pallas kernels: 6.14 us -> 5.19 us
    pallas_call x3, Pallas kernels: 2.91 us -> 2.08 us  [local(): call(functools.partial(turn_kernel, plan, factors), [VMEM] * 6, [pay(plan...]
where the time goes in v3:
time: 56.1 us; the launch traced here: 55.8 us
  blocking collectives  49.9 us (89%)
  Pallas kernels  5.19 us (9%)
  between operations  0.7 us (1%)
    all_to_all x5, blocking collectives, exchange(): return lax.all_to_all(sent, AXES, 0, 0, tiled=True)  49.9 us
    pallas_call x3, Pallas kernels, local(): call(functools.partial(turn_kernel, plan, factors), [VMEM] * 6, [pay(plan...  2.08 us
    pallas_call x1, Pallas kernels, local(): call(functools.partial(closing_kernel, plan), [VMEM] * 5, [state, state],...  1.26 us

profile of v3, /device:TPU:0, one launch (start us, length us, event | category | flops | bytes accessed | tf_op | source)
XLA Modules:
  0.0 55.8 jit_solution(11483775865523631612)
XLA Ops:
  0.6 0.0 copy-start
  0.6 0.0 copy-start.1
  0.7 0.0 copy-start.2
  0.7 1.0 %shard_map.68 = (bf16[32,8,128]{2,1,0:T(8,128)(2,1)S(1)}, s32[1,128]{1,0:T(1,128)S(1)}) custom-call(s32[2,1,8]{2,1,0:T(1,128)} %order_hbm.1, s32[2,1,8,27]{3,2,1,0:T(8,128)} %pattern_hbm.1, f32[4,128]{1,0:T(4,128)} %bitcast.16), custom_call_target="tpu_custom_call" | custom-call | flops 10000000000 | bytes 100000000 | tf_op jit(solution)/shard_map/pallas_call | solution.py:282
  1.7 14.4 %all_to_all.25.received_ref = bf16[32,8,128]{2,1,0:T(8,128)(2,1)S(1)} all-to-all(bf16[32,8,128]{2,1,0:T(8,128)(2,1)S(1)} %get-tuple-element.22), channel_id=1, replica_groups=mesh['gx'=4,'gy'=2,'gz'=4] {'gz','gx','gy'}, dimensions={0} | all-to-all | bytes 131072 | tf_op jit(solution)/shard_map/all_to_all | solution.py:275
  16.1 0.0 copy-done
  16.1 0.0 copy-done.1
  16.1 0.0 copy-done.2
  16.1 0.8 %shard_map.69 = (bf16[32,4,128]{2,1,0:T(4,128)(2,1)S(1)}, bf16[160,128]{1,0:T(8,128)(2,1)S(1)}, f32[4,128]{1,0:T(4,128)S(1)}, f32[4,128]{1,0:T(4,128)S(1)}, f32[4,128]{1,0:T(4,128)S(1)}) custom-call(bf16[32,8,128]{2,1,0:T(8,128)(2,1)S(1)} %all_to_all.25.received_ref, bf16[2,1,2,27,128,128]{5,4,3,2,1,0:T(8,128)(2,1)S(1)} %copy-done, ...), custom_call_target="tpu_custom_call" | custom-call | tf_op jit(solution)/shard_map/pallas_call | solution.py:294
  16.9 8.9 %all_to_all.26 = bf16[32,4,128]{2,1,0:T(4,128)(2,1)S(1)} all-to-all(bf16[32,4,128]{2,1,0:T(4,128)(2,1)S(1)} %get-tuple-element.24), channel_id=1, replica_groups=mesh['gx'=4,'gy'=2,'gz'=4] {'gz','gx','gy'}, dimensions={0} | all-to-all | bytes 65536 | tf_op jit(solution)/shard_map/all_to_all | solution.py:275
  25.8 0.7 %shard_map.70 = (bf16[32,4,128]{2,1,0:T(4,128)(2,1)S(1)}, f32[4,128]{1,0:T(4,128)S(1)}, f32[4,128]{1,0:T(4,128)S(1)}, f32[4,128]{1,0:T(4,128)S(1)}) custom-call(bf16[128,128]{1,0:T(8,128)(2,1)S(1)} %bitcast.12, bf16[2,1,2,27,128,128]{5,4,3,2,1,0:T(8,128)(2,1)S(1)} %copy-done, bf16[160,128]{1,0:T(8,128)(2,1)S(1)} %get-tuple-element.25.select_ref, ...), custom_call_target="tpu_custom_call" | custom-call | tf_op jit(solution)/shard_map/pallas_call | solution.py:308
  26.5 8.9 %all_to_all.27 = bf16[32,4,128]{2,1,0:T(4,128)(2,1)S(1)} all-to-all(bf16[32,4,128]{2,1,0:T(4,128)(2,1)S(1)} %get-tuple-element.29), channel_id=1, replica_groups=mesh['gx'=4,'gy'=2,'gz'=4] {'gz','gx','gy'}, dimensions={0} | all-to-all | bytes 65536 | tf_op jit(solution)/shard_map/all_to_all | solution.py:275
  35.4 0.7 %shard_map.71 = (bf16[32,4,128]{2,1,0:T(4,128)(2,1)S(1)}, f32[4,128]{1,0:T(4,128)S(1)}, f32[4,128]{1,0:T(4,128)S(1)}, f32[4,128]{1,0:T(4,128)S(1)}) custom-call(bf16[128,128]{1,0:T(8,128)(2,1)S(1)} %bitcast.13, bf16[2,1,2,27,128,128]{5,4,3,2,1,0:T(8,128)(2,1)S(1)} %copy-done, bf16[160,128]{1,0:T(8,128)(2,1)S(1)} %get-tuple-element.25.select_ref, ...), custom_call_target="tpu_custom_call" | custom-call | tf_op jit(solution)/shard_map/pallas_call | solution.py:308
  36.1 8.9 %all_to_all.28 = bf16[32,4,128]{2,1,0:T(4,128)(2,1)S(1)} all-to-all(bf16[32,4,128]{2,1,0:T(4,128)(2,1)S(1)} %get-tuple-element.33), channel_id=1, replica_groups=mesh['gx'=4,'gy'=2,'gz'=4] {'gz','gx','gy'}, dimensions={0} | all-to-all | bytes 65536 | tf_op jit(solution)/shard_map/all_to_all | solution.py:275
  45.0 0.7 %shard_map.72 = (bf16[32,4,128]{2,1,0:T(4,128)(2,1)S(1)}, f32[4,128]{1,0:T(4,128)S(1)}, f32[4,128]{1,0:T(4,128)S(1)}) custom-call(bf16[128,128]{1,0:T(8,128)(2,1)S(1)} %bitcast.14, bf16[2,1,2,27,128,128]{5,4,3,2,1,0:T(8,128)(2,1)S(1)} %copy-done, bf16[160,128]{1,0:T(8,128)(2,1)S(1)} %get-tuple-element.25.select_ref, ...), custom_call_target="tpu_custom_call" | custom-call | tf_op jit(solution)/shard_map/pallas_call | solution.py:308
  45.7 8.9 %all_to_all.29 = bf16[32,4,128]{2,1,0:T(4,128)(2,1)S(1)} all-to-all(bf16[32,4,128]{2,1,0:T(4,128)(2,1)S(1)} %get-tuple-element.37), channel_id=1, replica_groups=mesh['gx'=4,'gy'=2,'gz'=4] {'gz','gx','gy'}, dimensions={0} | all-to-all | bytes 65536 | tf_op jit(solution)/shard_map/all_to_all | solution.py:275
  54.6 1.3 %shard_map.73 = (f32[4,128]{1,0:T(4,128)}, f32[4,128]{1,0:T(4,128)}) custom-call(bf16[128,128]{1,0:T(8,128)(2,1)S(1)} %bitcast.15, bf16[2,1,2,27,128,128]{5,4,3,2,1,0:T(8,128)(2,1)S(1)} %copy-done, bf16[160,128]{1,0:T(8,128)(2,1)S(1)} %get-tuple-element.25.select_ref, f32[4,128]{1,0:T(4,128)S(1)} %get-tuple-element.38.smoothed_in, ...), custom_call_target="tpu_custom_call" | custom-call | tf_op jit(solution)/shard_map/pallas_call | solution.py:314
Async XLA Ops:
  0.6 15.5 %copy-start = (bf16[2,1,2,27,128,128]{5,4,3,2,1,0:T(8,128)(2,1)S(1)}, bf16[2,1,2,27,128,128]{5,4,3,2,1,0:T(8,128)(2,1)}, u32[]{:S(2)}) copy-start(bf16[2,1,2,27,128,128]{5,4,3,2,1,0:T(8,128)(2,1)} %blocks_ref.9) | copy-start | bytes 10616836
  0.6 15.5 %copy-start.1 = (f32[2,1,2,128]{3,2,1,0:T(2,128)S(1)}, f32[2,1,2,128]{3,2,1,0:T(2,128)}, u32[]{:S(2)}) copy-start(f32[2,1,2,128]{3,2,1,0:T(2,128)} %param.8) | copy-start | bytes 6148
  0.7 15.5 %copy-start.2 = (f32[2,1,2,128]{3,2,1,0:T(2,128)S(1)}, f32[2,1,2,128]{3,2,1,0:T(2,128)}, u32[]{:S(2)}) copy-start(f32[2,1,2,128]{3,2,1,0:T(2,128)} %param.9) | copy-start | bytes 6148

commit v4 on v3

--- a/solution.py
+++ b/solution.py
@@ -49,8 +49,12 @@
         self.spans = min(3, self.gy) if self.few else 3
         self.entries = [(i, j, k) for i in range(3) for j in range(self.spans) for k in range(3)]
         self.targets = -(-self.rows * PITCH // LANES) * LANES
-        self.lot = -(-self.rows // 8) * 8
-        self.half = -(-(len(self.entries) + 1) // 2 * self.lot // 16) * 16
+        self.tiled = list(range(self.rows // 4))
+        self.plain = list(range(self.rows // 4, self.rows))
+        self.quads = -(-len(self.entries) // 4)
+        self.half = 8 * self.quads * len(self.tiled)
+        lines = 2 * self.half + len(self.plain) * len(self.entries)
+        self.lines = -(-lines // 16) * 16
 
     def first_span(self):
         return 1 - lax.axis_index("gy") if self.few else 0
@@ -58,8 +62,13 @@
     def place(self, row):
         return row // (self.ny * self.nz), row // self.nz % self.ny, row % self.nz
 
-    def spot(self, number):
-        return number % 2 * self.half + number // 2 * self.lot
+    def lot(self, row, quad, side):
+        return side * self.half + 8 * (row * self.quads + quad)
+
+    def spot(self, row, number):
+        if row in self.tiled:
+            return self.lot(row, number // 4, number % 2) + number % 4 // 2
+        return 2 * self.half + (row - len(self.tiled)) * len(self.entries) + number
 
     def key(self, x, y, z):
         return ((x + 1) * (self.gy * self.ny + 2) + y + 1) * (self.gz * self.nz + 2) + z + 1
@@ -109,9 +118,7 @@
         flags = pattern_ref[x, y, pl.ds(first + s, 1), :]
         gap = jnp.zeros((1, plan.targets - flags.shape[1]), jnp.int32)
         flags = jnp.concatenate([flags, gap], axis=1)
-        keep = keep + (pltpu.roll(flags, PITCH * number, 1) if number else flags)
-    if plan.few:
-        keep = jnp.where(span == 1, pltpu.roll(keep, plan.targets - 3, 1), keep)
+        keep = keep + pltpu.roll(flags, lax.rem(plan.targets + PITCH * number - 3 * span, plan.targets), 1)
     b = b + span
     keep = ((keep > 0) | (9 * a + 3 * b + c == 13)) & (entry < 27) & (row < plan.rows)
     xy, _ = split(row, plan.nz)
@@ -139,80 +146,85 @@
         for first in range(0, plan.targets, LANES):
             part = slice(first, first + LANES)
             table_ref[part, :] = jnp.where(have[some] == want[:, part], 1.0, 0.0).T
-        for number, (i, j, k) in enumerate(plan.entries):
-            rows = table_ref[pl.ds(9 * i + 3 * j + k, plan.rows, stride=PITCH), :]
-            at = plan.spot(number)
-            wide_ref[at : at + plan.rows, some] = rows
+        for row in range(plan.rows):
+            for number, (i, j, k) in enumerate(plan.entries):
+                line = PITCH * row + 9 * i + 3 * j + k
+                at = plan.spot(row, number)
+                wide_ref[at : at + 1, some] = table_ref[line : line + 1, :]
     select_ref[...] = wide_ref[...].astype(jnp.bfloat16)
 
 
-def product(plan, blocks_ref, rows_ref, select_ref, gather_ref):
+def product(plan, blocks_ref, wide_ref, rows_ref, select_ref, gather_ref, opening=False):
     gather_ref[...] = jnp.dot(select_ref[...], rows_ref[...], preferred_element_type=jnp.float32)
     span = plan.first_span()
     size = plan.width
+    count = len(plan.entries)
 
     def block(row, number):
         x, y, s = plan.place(row)
         i, j, k = plan.entries[number]
         return blocks_ref[x, y, s, 9 * i + 3 * (j + span) + k]
 
-    results = [None] * plan.rows
-    count = len(plan.entries) // 2
-    for low in range(0, plan.rows // 4 * 2, 2):
-        sums = []
-        for part in (range(0, count // 2), range(count // 2, count)):
+    def pair(row, number):
+        blank = jnp.zeros((size, size), jnp.bfloat16)
+        sides = [block(row, at) if at < count else blank for at in (number, number + 1)]
+        return jnp.concatenate(sides, axis=1)
+
+    results = []
+    for row in plan.tiled:
+        found = jnp.zeros((1, size), jnp.float32)
+        whole = [quad for quad in range(plan.quads) if 4 * quad + 2 < count]
+        cut = len(whole) // 2
+        for group in (whole[:cut], whole[cut:], [plan.quads - 1] if plan.quads > len(whole) else []):
+            if not group:
+                continue
             left, right = [], []
-            for pair in part:
+            for quad in group:
                 for side in (0, 1):
-                    at = plan.spot(2 * pair + side)
-                    left.append(gather_ref[at : at + plan.lot, :].astype(jnp.bfloat16))
-                    right.append(
-                        jnp.concatenate([block(row, 2 * pair + side) for row in (low, low + 1)], axis=0)
-                    )
-            sums.append(
-                lax.dot_general(
-                    jnp.concatenate(left, axis=1),
-                    jnp.concatenate(right, axis=1),
-                    (((1,), (1,)), ((), ())),
-                    preferred_element_type=jnp.float32,
-                )
+                    at = plan.lot(row, quad, side)
+                    left.append(gather_ref[at : at + 8, :].astype(jnp.bfloat16))
+                parts = [pair(row, at) for at in (4 * quad, 4 * quad + 2) if at < count]
+                right.append(jnp.concatenate(parts, axis=0))
+            both = lax.dot_general(
+                jnp.concatenate(left, axis=1),
+                jnp.concatenate(right, axis=1),
+                (((1,), (1,)), ((), ())),
+                preferred_element_type=jnp.float32,
             )
-        both = sums[0] + sums[1]
-        results[low] = both[low : low + 1, :size]
-        results[low + 1] = both[low + 1 : low + 2, size:]
-
+            found = found + both[:1, :size]
+            if both.shape[1] > size:
+                found = found + both[1:2, size:]
+        results.append(found)
     lane = lax.broadcasted_iota(jnp.int32, (size, size), 1)
     line = lax.broadcasted_iota(jnp.int32, (size, size), 0)
-    for row in range(plan.rows):
-        if results[row] is None:
-            numbers = range(len(plan.entries))
-        else:
-            numbers = range(2 * count, len(plan.entries))
-        if not numbers:
-            continue
+    for place, row in enumerate(plan.plain):
         total = jnp.zeros((size, size), jnp.float32)
-        for number in numbers:
-            at = plan.spot(number) + row
-            total = total + block(row, number).astype(jnp.float32) * gather_ref[at : at + 1, :]
+        for number in range(count):
+            at = plan.spot(row, number)
+            if opening:
+                values = block(row, number).astype(jnp.float32)
+                wide_ref[place, number] = values
+            else:
+                values = wide_ref[place, number]
+            total = total + values * gather_ref[at : at + 1, :]
         sums = jnp.sum(total, axis=1, keepdims=True)
-        found = jnp.sum(jnp.where(lane == line, sums, 0.0), axis=0, keepdims=True)
-        results[row] = found if results[row] is None else results[row] + found
+        results.append(jnp.sum(jnp.where(lane == line, sums, 0.0), axis=0, keepdims=True))
     return jnp.concatenate(results, axis=0)
 
 
 def opening_kernel(
     plan, received_ref, blocks_ref, want_ref, start_ref, rhs_ref,
-    pay_ref, select_ref, smoothed_ref, remainder_ref, search_ref,
-    gather_ref, stage_ref, rows_ref, table_ref, wide_ref,
+    pay_ref, select_ref, wide_ref, smoothed_ref, remainder_ref, search_ref,
+    gather_ref, stage_ref, rows_ref, table_ref, spread_ref,
 ):
     for device in range(plan.devices):
         here = slice(device * plan.rows, (device + 1) * plan.rows)
         values = received_ref[device].astype(jnp.float32)
         rows_ref[here, :] = values[: plan.rows]
         stage_ref[here, :] = values[plan.rows :]
-    selection(plan, stage_ref[...].astype(jnp.int32), want_ref[...], table_ref, wide_ref, select_ref)
+    selection(plan, stage_ref[...].astype(jnp.int32), want_ref[...], table_ref, spread_ref, select_ref)
     remainder = rhs_ref[...] - product(
-        plan, blocks_ref, Rounded(rows_ref), select_ref, gather_ref
+        plan, blocks_ref, wide_ref, Rounded(rows_ref), select_ref, gather_ref, opening=True
     )
     search = remainder / CENTER
     send(search, pay_ref)
@@ -222,11 +234,13 @@
 
 
 def turn_kernel(
-    plan, factors, received_ref, blocks_ref, select_ref, smoothed_in, remainder_in, search_in,
+    plan, factors, received_ref, blocks_ref, wide_ref, select_ref, smoothed_in, remainder_in, search_in,
     pay_ref, smoothed_ref, remainder_ref, *rest,
 ):
     *search_ref, gather_ref = rest
-    remainder = remainder_in[...] - product(plan, blocks_ref, received_ref, select_ref, gather_ref)
+    remainder = remainder_in[...] - product(
+        plan, blocks_ref, wide_ref, received_ref, select_ref, gather_ref
+    )
     search = factors[0] * search_in[...] + factors[1] * remainder
     send(search, pay_ref)
     remainder_ref[...] = remainder
@@ -236,25 +250,25 @@
 
 
 def closing_kernel(
-    plan, received_ref, blocks_ref, select_ref, smoothed_in, remainder_in,
+    plan, received_ref, blocks_ref, wide_ref, select_ref, smoothed_in, remainder_in,
     smoothed_ref, remainder_ref, gather_ref,
 ):
     smoothed_ref[...] = smoothed_in[...]
     remainder_ref[...] = remainder_in[...] - product(
-        plan, blocks_ref, received_ref, select_ref, gather_ref
+        plan, blocks_ref, wide_ref, received_ref, select_ref, gather_ref
     )
 
 
 def local(blocks, pattern, order, start, rhs):
     plan = Plan([lax.axis_size(axis) for axis in ("gx", "gy", "gz")], start.shape)
     state = jax.ShapeDtypeStruct((plan.rows, plan.width), jnp.float32)
-    select = jax.ShapeDtypeStruct((2 * plan.half, plan.sources), jnp.bfloat16)
-    gather = [pltpu.VMEM((2 * plan.half, plan.width), jnp.float32)]
+    select = jax.ShapeDtypeStruct((plan.lines, plan.sources), jnp.bfloat16)
+    gather = [pltpu.VMEM((plan.lines, plan.width), jnp.float32)]
     tables = [
         pltpu.VMEM((plan.sources, plan.width), jnp.float32),
         pltpu.VMEM((plan.sources, plan.width), jnp.float32),
         pltpu.VMEM((plan.targets, LANES), jnp.float32),
-        pltpu.VMEM((2 * plan.half, plan.sources), jnp.float32),
+        pltpu.VMEM((plan.lines, plan.sources), jnp.float32),
     ]
 
     def pay(rows):
@@ -291,10 +305,12 @@
         ],
         pl.CostEstimate(flops=10**10, bytes_accessed=10**8, transcendentals=0),
     )(far(order), far(pattern), far(flat_start))
-    sent, table, smoothed, remainder, search = call(
+    wide = (len(plan.plain), len(plan.entries), plan.width, plan.width)
+    wide = jax.ShapeDtypeStruct(wide, jnp.float32)
+    sent, table, wide, smoothed, remainder, search = call(
         functools.partial(opening_kernel, plan),
         [VMEM] * 5,
-        [pay(plan.rows), select, state, state, state],
+        [pay(plan.rows), select, wide, state, state, state],
         gather + tables,
     )(exchange(sent), blocks, want, flat_start, flat_rhs)
     sigma = CENTER / SPREAD
@@ -307,13 +323,13 @@
         states = [state] * (3 if number + 2 < DEG else 2)
         sent, smoothed, remainder, *search = call(
             functools.partial(turn_kernel, plan, factors),
-            [VMEM] * 6,
+            [VMEM] * 7,
             [pay(plan.rows)] + states,
             gather,
-        )(packed(exchange(sent)), blocks, table, smoothed, remainder, *search)
+        )(packed(exchange(sent)), blocks, wide, table, smoothed, remainder, *search)
     smoothed, remainder = call(
-        functools.partial(closing_kernel, plan), [VMEM] * 5, [state, state], gather
-    )(packed(exchange(sent)), blocks, table, smoothed, remainder)
+        functools.partial(closing_kernel, plan), [VMEM] * 6, [state, state], gather
+    )(packed(exchange(sent)), blocks, wide, table, smoothed, remainder)
     return smoothed.reshape(start.shape), remainder.reshape(start.shape)
 
 

time: 56.1 us -> 55.4 us (0.988)
  Pallas kernels: 5.19 us -> 4.52 us
    pallas_call x4, Pallas kernels: 3.34 us -> 2.75 us  [the longest x3 1.63 us: local(): call(functools.partial(turn_kernel, plan, factors), [VMEM] * 7, [pay(plan...]
where the time goes in v4:
time: 55.4 us; the launch traced here: 55.2 us
  blocking collectives  49.9 us (90%)
  Pallas kernels  4.52 us (8%)
  between operations  0.7 us (1%)
    all_to_all x5, blocking collectives, exchange(): return lax.all_to_all(sent, AXES, 0, 0, tiled=True)  49.9 us
    pallas_call x3, Pallas kernels, local(): call(functools.partial(turn_kernel, plan, factors), [VMEM] * 7, [pay(plan...  1.63 us
    pallas_call x1, Pallas kernels, local(): call(functools.partial(closing_kernel, plan), [VMEM] * 6, [state, state],...  1.12 us

profile of v4, /device:TPU:0, one launch (start us, length us, event | category | flops | bytes accessed | tf_op | source)
XLA Modules:
  0.0 55.2 jit_solution(8857671485330377398)
XLA Ops:
  0.6 0.0 copy-start
  0.6 0.0 copy-start.1
  0.7 0.0 copy-start.2
  0.7 1.0 %shard_map.68 = (bf16[32,8,128]{2,1,0:T(8,128)(2,1)S(1)}, s32[1,128]{1,0:T(1,128)S(1)}) custom-call(s32[2,1,8]{2,1,0:T(1,128)} %order_hbm.1, s32[2,1,8,27]{3,2,1,0:T(8,128)} %pattern_hbm.1, f32[4,128]{1,0:T(4,128)} %bitcast.16), custom_call_target="tpu_custom_call" | custom-call | flops 10000000000 | bytes 100000000 | tf_op jit(solution)/shard_map/pallas_call | solution.py:296
  1.6 14.4 %all_to_all.25.received_ref = bf16[32,8,128]{2,1,0:T(8,128)(2,1)S(1)} all-to-all(bf16[32,8,128]{2,1,0:T(8,128)(2,1)S(1)} %get-tuple-element.23), channel_id=1, replica_groups=mesh['gx'=4,'gy'=2,'gz'=4] {'gz','gx','gy'}, dimensions={0} | all-to-all | bytes 131072 | tf_op jit(solution)/shard_map/all_to_all | solution.py:289
  16.0 0.0 copy-done
  16.0 0.0 copy-done.1
  16.0 0.0 copy-done.2
  16.1 0.8 %shard_map.69 = (bf16[32,4,128]{2,1,0:T(4,128)(2,1)S(1)}, bf16[144,128]{1,0:T(8,128)(2,1)S(1)}, f32[3,18,128,128]{3,2,1,0:T(8,128)S(1)}, f32[4,128]{1,0:T(4,128)...) custom-call(bf16[32,8,128]{2,1,0:T(8,128)(2,1)S(1)} %all_to_all.25.received_ref, ...), custom_call_target="tpu_custom_call" | custom-call | tf_op jit(solution)/shard_map/pallas_call | solution.py:310
  16.9 8.9 %all_to_all.26 = bf16[32,4,128]{2,1,0:T(4,128)(2,1)S(1)} all-to-all(bf16[32,4,128]{2,1,0:T(4,128)(2,1)S(1)} %get-tuple-element.25), channel_id=1, replica_groups=mesh['gx'=4,'gy'=2,'gz'=4] {'gz','gx','gy'}, dimensions={0} | all-to-all | bytes 65536 | tf_op jit(solution)/shard_map/all_to_all | solution.py:289
  25.8 0.5 shard_map.70
  26.3 8.9 %all_to_all.27 = bf16[32,4,128]{2,1,0:T(4,128)(2,1)S(1)} all-to-all(bf16[32,4,128]{2,1,0:T(4,128)(2,1)S(1)} %get-tuple-element.31), channel_id=1, replica_groups=mesh['gx'=4,'gy'=2,'gz'=4] {'gz','gx','gy'}, dimensions={0} | all-to-all | bytes 65536 | tf_op jit(solution)/shard_map/all_to_all | solution.py:289
  35.2 0.5 shard_map.71
  35.7 8.9 %all_to_all.28 = bf16[32,4,128]{2,1,0:T(4,128)(2,1)S(1)} all-to-all(bf16[32,4,128]{2,1,0:T(4,128)(2,1)S(1)} %get-tuple-element.35), channel_id=1, replica_groups=mesh['gx'=4,'gy'=2,'gz'=4] {'gz','gx','gy'}, dimensions={0} | all-to-all | bytes 65536 | tf_op jit(solution)/shard_map/all_to_all | solution.py:289
  44.6 0.5 shard_map.72
  45.2 8.9 %all_to_all.29 = bf16[32,4,128]{2,1,0:T(4,128)(2,1)S(1)} all-to-all(bf16[32,4,128]{2,1,0:T(4,128)(2,1)S(1)} %get-tuple-element.39), channel_id=1, replica_groups=mesh['gx'=4,'gy'=2,'gz'=4] {'gz','gx','gy'}, dimensions={0} | all-to-all | bytes 65536 | tf_op jit(solution)/shard_map/all_to_all | solution.py:289
  54.1 1.1 %shard_map.73 = (f32[4,128]{1,0:T(4,128)}, f32[4,128]{1,0:T(4,128)}) custom-call(bf16[128,128]{1,0:T(8,128)(2,1)S(1)} %bitcast.15, bf16[2,1,2,27,128,128]{5,4,3,2,1,0:T(8,128)(2,1)S(1)} %copy-done, f32[3,18,128,128]{3,2,1,0:T(8,128)S(1)} %get-tuple-element.26.wide_ref, bf16[144,128]{1,0:T(8,128)(2,1)S(1)} %get-tuple-element.27.select_ref, ...), custom_call_target="tpu_custom_call" | custom-call | tf_op jit(solution)/shard_map/pallas_call | solution.py:330
Async XLA Ops:
  0.6 15.4 %copy-start = (bf16[2,1,2,27,128,128]{5,4,3,2,1,0:T(8,128)(2,1)S(1)}, bf16[2,1,2,27,128,128]{5,4,3,2,1,0:T(8,128)(2,1)}, u32[]{:S(2)}) copy-start(bf16[2,1,2,27,128,128]{5,4,3,2,1,0:T(8,128)(2,1)} %blocks_ref.9) | copy-start | bytes 10616836
  0.6 15.4 %copy-start.1 = (f32[2,1,2,128]{3,2,1,0:T(2,128)S(1)}, f32[2,1,2,128]{3,2,1,0:T(2,128)}, u32[]{:S(2)}) copy-start(f32[2,1,2,128]{3,2,1,0:T(2,128)} %param.8) | copy-start | bytes 6148
  0.7 15.4 %copy-start.2 = (f32[2,1,2,128]{3,2,1,0:T(2,128)S(1)}, f32[2,1,2,128]{3,2,1,0:T(2,128)}, u32[]{:S(2)}) copy-start(f32[2,1,2,128]{3,2,1,0:T(2,128)} %param.9) | copy-start | bytes 6148

commit v5 on v4

v5 whole, which is shorter than its diff:
```python
import functools

import jax
import jax.numpy as jnp
from jax import lax
from jax.experimental import pallas as pl
from jax.experimental.pallas import tpu as pltpu
from jax.sharding import PartitionSpec as P

DEG = 4
CENTER = 1.0
SPREAD = 0.8
LANES = 128
PITCH = 32
GRANT = 16 * 2**20
AXES = ("gz", "gx", "gy")
VMEM = pl.BlockSpec(memory_space=pltpu.VMEM)
HBM = pl.BlockSpec(memory_space=pltpu.HBM)


def far(array):
    return pltpu.with_memory_space_constraint(array, pltpu.HBM)


class Plan:
    def __init__(self, axis_sizes, local_shape):
        self.gx, self.gy, self.gz = axis_sizes
        self.nx, self.ny, self.nz, self.width = local_shape
        self.devices = self.gx * self.gy * self.gz
        self.rows = self.nx * self.ny * self.nz
        self.sources = self.devices * self.rows
        self.few = self.ny == 1 and self.gy <= 2
        self.spans = min(3, self.gy) if self.few else 3
        self.entries = [(i, j, k) for i in range(3) for j in range(self.spans) for k in range(3)]
        self.targets = -(-self.rows * PITCH // LANES) * LANES
        self.tiled = list(range(self.rows // 4))
        self.plain = list(range(self.rows // 4, self.rows))
        self.quads = -(-len(self.entries) // 4)
        self.depth = self.gz * self.nz
        self.high = -(-self.depth // 8) * 8
        self.across = self.spans if self.few else self.ny + 2
        self.columns = (self.nx + 2) * self.across
        self.picks = [
            (row, i, j) for row in range(self.rows) for i in range(3) for j in range(self.spans)
        ]

    def first_span(self):
        return 1 - lax.axis_index("gy") if self.few else 0

    def place(self, row):
        return row // (self.ny * self.nz), row // self.nz % self.ny, row % self.nz

    def spot(self, row, number):
        i, j, k = self.entries[number]
        return 8 * ((row * 3 + i) * self.spans + j) + k

    def column(self, row, i, j):
        x, y, _ = self.place(row)
        return (x + i) * self.across + (j if self.few else y + j)

    def beside(self, number, count, axis, devices):
        me = lax.axis_index(axis)
        if number == 0:
            return jnp.maximum(me - 1, 0), count - 1, me > 0
        if number == count + 1:
            return jnp.minimum(me + 1, devices - 1), 0, me < devices - 1
        return me, number - 1, None


def send(tile, pay_ref):
    pay_ref[...] = jnp.broadcast_to(tile.astype(jnp.bfloat16)[None], pay_ref.shape)


def first_kernel(
    plan, order_hbm, pattern_hbm, start_hbm,
    pay_ref, plane_ref, keep_ref, start_ref, order_ref, pattern_ref, sems,
):
    copies = (
        pltpu.make_async_copy(order_hbm, order_ref, sems.at[0]),
        pltpu.make_async_copy(pattern_hbm, pattern_ref, sems.at[1]),
        pltpu.make_async_copy(start_hbm, start_ref, sems.at[2]),
    )
    for copy in copies:
        copy.start()
    for copy in copies:
        copy.wait()
    first = lax.axis_index("gz") * plan.nz
    line = lax.broadcasted_iota(jnp.int32, (plan.rows, plan.width), 0)
    planes = jnp.zeros_like(line)
    for row in range(plan.rows):
        x, y, s = plan.place(row)
        planes = jnp.where(line == row, order_ref[x, y, first + s], planes)
    planes = planes.astype(jnp.float32)
    send(jnp.concatenate([start_ref[...], planes], axis=0), pay_ref)
    plane_ref[...] = planes
    keep_ref[...] = kept(plan, pattern_ref)


def kept(plan, pattern_ref):
    first = lax.axis_index("gz") * plan.nz
    span = plan.first_span()
    lane = lax.broadcasted_iota(jnp.int32, (1, plan.targets), 1)
    flat = jnp.zeros_like(lane)
    for number in range(plan.rows):
        x, y, s = plan.place(number)
        flags = pattern_ref[x, y, pl.ds(first + s, 1), :]
        gap = jnp.zeros((1, plan.targets - flags.shape[1]), jnp.int32)
        flags = jnp.concatenate([flags, gap], axis=1)
        turn = lax.rem(plan.targets + PITCH * number - 3 * span, plan.targets)
        flat = flat + pltpu.roll(flags, turn, 1)
    centre = (lane & (PITCH - 1)) + 3 * span == 13
    return jnp.where((flat > 0) | centre, 1.0, 0.0)


def gathered_columns(plan, received_ref, base):
    loaded = {}
    columns = []
    for i in range(plan.nx + 2):
        device_x, x, _ = plan.beside(i, plan.nx, "gx", plan.gx)
        side = (i > 0) + (i > plan.nx)
        for j in range(plan.across):
            if plan.few:
                device_y, y, slice_y = j, 0, j
            else:
                device_y, y, _ = plan.beside(j, plan.ny, "gy", plan.gy)
                slice_y = (j > 0) + (j > plan.ny)
            parts = []
            for z in range(plan.gz):
                name = (side, slice_y, z)
                if name not in loaded:
                    device = (z * plan.gx + device_x) * plan.gy + device_y
                    loaded[name] = received_ref[device].astype(jnp.float32)
                low = base + (x * plan.ny + y) * plan.nz
                parts.append(loaded[name][low : low + plan.nz])
            if plan.high > plan.depth:
                parts.append(jnp.zeros((plan.high - plan.depth, plan.width), jnp.float32))
            columns.append(jnp.concatenate(parts, axis=0))
    return columns


def pick(column, index):
    high = column.shape[0]
    numbers = lax.GatherDimensionNumbers(
        offset_dims=(),
        collapsed_slice_dims=(0,),
        start_index_map=(0,),
        operand_batching_dims=(1,),
        start_indices_batching_dims=(1,),
    )
    found = None
    for group in range(high // 8):
        part = lax.gather(
            column[8 * group : 8 * group + 8],
            (index if high == 8 else index & 7)[..., None],
            numbers,
            (1, 1),
            mode=lax.GatherScatterMode.PROMISE_IN_BOUNDS,
        )
        found = part if found is None else jnp.where(index >> 3 == group, part, found)
    return found


def tables(plan, columns, plane_ref, keep_ref, slots_ref, flags_ref, index_ref, mask_ref):
    for first in range(0, plan.targets, LANES):
        part = jnp.broadcast_to(keep_ref[:, first : first + LANES], (LANES, LANES))
        flags_ref[first : first + LANES, :] = part.T
    line = lax.broadcasted_iota(jnp.int32, (plan.high, LANES), 0).astype(jnp.float32)
    inverses = []
    for number, column in enumerate(columns):
        slots_ref[number] = column
        inverse = jnp.zeros((plan.high, LANES), jnp.int32)
        for slot in range(plan.depth):
            inverse = jnp.where(slots_ref[number, slot : slot + 1, :] == line, slot, inverse)
        inverses.append(inverse)
    step = lax.broadcasted_iota(jnp.int32, (8, LANES), 0).astype(jnp.float32) - 1.0
    for place, (row, i, j) in enumerate(plan.picks):
        x, y, _ = plan.place(row)
        want = plane_ref[row : row + 1, :] + step
        inside = (want >= 0.0) & (want < plan.depth) & (step < 2.0)
        want = jnp.clip(want, 0.0, plan.depth - 1.0).astype(jnp.int32)
        at = row * PITCH + 9 * i + 3 * j
        mask = jnp.where(inside, flags_ref[at : at + 8, :], 0.0)
        _, _, on_grid = plan.beside(x + i, plan.nx, "gx", plan.gx)
        if on_grid is not None:
            mask = jnp.where(on_grid, mask, 0.0)
        if not plan.few:
            _, _, on_grid = plan.beside(y + j, plan.ny, "gy", plan.gy)
            if on_grid is not None:
                mask = jnp.where(on_grid, mask, 0.0)
        at = 8 * place
        index_ref[at : at + 8, :] = pick(inverses[plan.column(row, i, j)], want)
        mask_ref[at : at + 8, :] = mask


def block_of(plan, blocks_ref, row, number):
    x, y, s = plan.place(row)
    i, j, k = plan.entries[number]
    return blocks_ref[x, y, s, 9 * i + 3 * (j + plan.first_span()) + k]


def product(plan, blocks_ref, wide_ref, received_ref, index_ref, mask_ref, gather_ref, opening=False):
    columns = gathered_columns(plan, received_ref, 0)
    for place, (row, i, j) in enumerate(plan.picks):
        here = slice(8 * place, 8 * place + 8)
        values = pick(columns[plan.column(row, i, j)], index_ref[here, :])
        gather_ref[here, :] = values * mask_ref[here, :]
    size = plan.width
    count = len(plan.entries)
    block = functools.partial(block_of, plan, blocks_ref)

    def pair(row, number):
        blank = jnp.zeros((size, size), jnp.bfloat16)
        sides = [block(row, at) if at < count else blank for at in (number, number + 1)]
        return jnp.concatenate(sides, axis=1)

    def vectors(row, number):
        if number >= count:
            return jnp.zeros((1, size), jnp.float32)
        at = plan.spot(row, number)
        return gather_ref[at : at + 1, :]

    results = []
    for row in plan.tiled:
        found = jnp.zeros((1, size), jnp.float32)
        whole = [quad for quad in range(plan.quads) if 4 * quad + 2 < count]
        cut = len(whole) // 2
        for group in (whole[:cut], whole[cut:], [plan.quads - 1] if plan.quads > len(whole) else []):
            if not group:
                continue
            left, right = [], []
            for quad in group:
                for side in (0, 1):
                    lines = [vectors(row, 4 * quad + side), vectors(row, 4 * quad + 2 + side)]
                    left.append(jnp.concatenate(lines, axis=0).astype(jnp.bfloat16))
                parts = [pair(row, at) for at in (4 * quad, 4 * quad + 2) if at < count]
                right.append(jnp.concatenate(parts, axis=0))
            both = lax.dot_general(
                jnp.concatenate(left, axis=1),
                jnp.concatenate(right, axis=1),
                (((1,), (1,)), ((), ())),
                preferred_element_type=jnp.float32,
            )
            found = found + both[:1, :size]
            if both.shape[1] > size:
                found = found + both[1:2, size:]
        results.append(found)
    lane = lax.broadcasted_iota(jnp.int32, (size, size), 1)
    line = lax.broadcasted_iota(jnp.int32, (size, size), 0)
    for place, row in enumerate(plan.plain):
        total = jnp.zeros((size, size), jnp.float32)
        for number in range(count):
            if opening:
                values = block(row, number).astype(jnp.float32)
                wide_ref[place, number] = values
            else:
                values = wide_ref[place, number]
            total = total + values * vectors(row, number)
        sums = jnp.sum(total, axis=1, keepdims=True)
        results.append(jnp.sum(jnp.where(lane == line, sums, 0.0), axis=0, keepdims=True))
    return jnp.concatenate(results, axis=0)


def opening_kernel(
    plan, received_ref, blocks_ref, plane_ref, keep_ref, start_ref, rhs_ref,
    pay_ref, index_ref, mask_ref, wide_ref, smoothed_ref, remainder_ref, search_ref,
    gather_ref, slots_ref, flags_ref,
):
    columns = gathered_columns(plan, received_ref, plan.rows)
    tables(plan, columns, plane_ref, keep_ref, slots_ref, flags_ref, index_ref, mask_ref)
    remainder = rhs_ref[...] - product(
        plan, blocks_ref, wide_ref, received_ref, index_ref, mask_ref, gather_ref, True
    )
    search = remainder / CENTER
    send(search, pay_ref)
    remainder_ref[...] = remainder
    search_ref[...] = search
    smoothed_ref[...] = start_ref[...] + search


def turn_kernel(
    plan, factors, received_ref, blocks_ref, wide_ref, index_ref, mask_ref,
    smoothed_in, remainder_in, search_in,
    pay_ref, smoothed_ref, remainder_ref, *rest,
):
    *search_ref, gather_ref = rest
    remainder = remainder_in[...] - product(
        plan, blocks_ref, wide_ref, received_ref, index_ref, mask_ref, gather_ref
    )
    search = factors[0] * search_in[...] + factors[1] * remainder
    send(search, pay_ref)
    remainder_ref[...] = remainder
    smoothed_ref[...] = smoothed_in[...] + search
    if search_ref:
        search_ref[0][...] = search


def closing_kernel(
    plan, received_ref, blocks_ref, wide_ref, index_ref, mask_ref, smoothed_in, remainder_in,
    smoothed_ref, remainder_ref, gather_ref,
):
    smoothed_ref[...] = smoothed_in[...]
    remainder_ref[...] = remainder_in[...] - product(
        plan, blocks_ref, wide_ref, received_ref, index_ref, mask_ref, gather_ref
    )


def local(blocks, pattern, order, start, rhs):
    plan = Plan([lax.axis_size(axis) for axis in ("gx", "gy", "gz")], start.shape)
    width = plan.width

    def like(kind, *shape):
        return jax.ShapeDtypeStruct(shape, kind)

    def pay(rows):
        return like(jnp.bfloat16, plan.devices, rows, width)

    state = like(jnp.float32, plan.rows, width)
    scratch = [pltpu.VMEM((8 * len(plan.picks), width), jnp.float32)]

    def call(kernel, ins, outs, scratch_shapes, cost=None):
        return pl.pallas_call(
            kernel,
            in_specs=ins,
            out_specs=[VMEM] * len(outs),
            out_shape=outs,
            scratch_shapes=scratch_shapes,
            compiler_params=pltpu.CompilerParams(vmem_limit_bytes=GRANT),
            cost_estimate=cost,
        )

    def exchange(sent):
        return lax.all_to_all(sent, AXES, 0, 0, tiled=True)

    flat_start = start.reshape(state.shape)
    flat_rhs = rhs.reshape(state.shape)
    sent, plane, keep = call(
        functools.partial(first_kernel, plan),
        [HBM, HBM, HBM],
        [pay(2 * plan.rows), state, like(jnp.float32, 1, plan.targets)],
        [
            pltpu.VMEM(state.shape, jnp.float32),
            pltpu.SMEM(order.shape, jnp.int32),
            pltpu.VMEM(pattern.shape, jnp.int32),
            pltpu.SemaphoreType.DMA((3,)),
        ],
        pl.CostEstimate(flops=10**10, bytes_accessed=10**8, transcendentals=0),
    )(far(order), far(pattern), far(flat_start))
    sent, index, mask, wide, smoothed, remainder, *search = call(
        functools.partial(opening_kernel, plan),
        [VMEM] * 6,
        [
            pay(plan.rows),
            like(jnp.int32, 8 * len(plan.picks), LANES),
            like(jnp.float32, 8 * len(plan.picks), LANES),
            like(jnp.float32, len(plan.plain), len(plan.entries), width, width),
            state,
            state,
            state,
        ],
        scratch
        + [
            pltpu.VMEM((plan.columns, plan.high, LANES), jnp.float32),
            pltpu.VMEM((plan.targets, LANES), jnp.float32),
        ],
    )(exchange(sent), blocks, plane, keep, flat_start, flat_rhs)
    sigma = CENTER / SPREAD
    rho = 1.0 / sigma
    for number in range(DEG - 1):
        following = 1.0 / (2.0 * sigma - rho)
        factors = (following * rho, 2.0 * following / SPREAD)
        rho = following
        states = [state] * (3 if number + 2 < DEG else 2)
        sent, smoothed, remainder, *search = call(
            functools.partial(turn_kernel, plan, factors),
            [VMEM] * 8,
            [pay(plan.rows)] + states,
            scratch,
        )(exchange(sent), blocks, wide, index, mask, smoothed, remainder, *search)
    smoothed, remainder = call(
        functools.partial(closing_kernel, plan), [VMEM] * 7, [state, state], scratch
    )(exchange(sent), blocks, wide, index, mask, smoothed, remainder)
    return smoothed.reshape(start.shape), remainder.reshape(start.shape)


def solution(mesh):
    in_specs = (
        P("gx", "gy", "gz", None, None, None),
        P("gx", "gy", None, None),
        P("gx", "gy", None),
        P("gx", "gy", "gz", None),
        P("gx", "gy", "gz", None),
    )
    out_specs = (P("gx", "gy", "gz", None), P("gx", "gy", "gz", None))
    return jax.shard_map(local, mesh=mesh, in_specs=in_specs, out_specs=out_specs, check_vma=False)
```

time: 55.4 us -> 55.3 us (level)
  no operation moved by 1% of the time
where the time goes in v5:
time: 55.3 us; the launch traced here: 55 us
  blocking collectives  49.9 us (90%)
  Pallas kernels  4.37 us (8%)
  between operations  0.7 us (1%)
    all_to_all x5, blocking collectives, exchange(): return lax.all_to_all(sent, AXES, 0, 0, tiled=True)  49.9 us
    pallas_call x3, Pallas kernels, local(): call(functools.partial(turn_kernel, plan, factors), [VMEM] * 8, [pay(plan...  1.58 us

profile of v5, /device:TPU:0, one launch (start us, length us, event | category | flops | bytes accessed | tf_op | source)
XLA Modules:
  0.0 55.0 jit_solution(7526778924983737599)
XLA Ops:
  0.6 0.0 copy-start
  0.6 0.0 copy-start.1
  0.7 0.0 copy-start.2
  0.7 1.0 %shard_map.68 = (bf16[32,8,128]{2,1,0:T(8,128)(2,1)S(1)}, f32[4,128]{1,0:T(4,128)S(1)}, f32[1,128]{1,0:T(1,128)S(1)}) custom-call(s32[2,1,8]{2,1,0:T(1,128)} %order_hbm.1, s32[2,1,8,27]{3,2,1,0:T(8,128)} %pattern_hbm.1, f32[4,128]{1,0:T(4,128)} %bitcast.8), custom_call_target="tpu_custom_call" | custom-call | flops 10000000000 | bytes 100000000 | tf_op jit(solution)/shard_map/pallas_call | solution.py:336
  1.6 14.4 %all_to_all.25.received_ref = bf16[32,8,128]{2,1,0:T(8,128)(2,1)S(1)} all-to-all(bf16[32,8,128]{2,1,0:T(8,128)(2,1)S(1)} %get-tuple-element.25), channel_id=1, replica_groups=mesh['gx'=4,'gy'=2,'gz'=4] {'gz','gx','gy'}, dimensions={0} | all-to-all | bytes 131072 | tf_op jit(solution)/shard_map/all_to_all | solution.py:332
  16.0 0.0 copy-done
  16.0 0.0 copy-done.1
  16.0 0.0 copy-done.2
  16.0 0.7 %shard_map.69 = (bf16[32,4,128]{2,1,0:T(4,128)(2,1)S(1)}, s32[192,128]{1,0:T(8,128)S(1)}, f32[192,128]{1,0:T(8,128)S(1)}, f32[3,18,128,128]{3,2,1,0:T(8,128)S(1)...) custom-call(bf16[32,8,128]{2,1,0:T(8,128)(2,1)S(1)} %all_to_all.25.received_ref, ...), custom_call_target="tpu_custom_call" | custom-call | tf_op jit(solution)/shard_map/pallas_call | solution.py:348
  16.8 8.9 %all_to_all.26.received_ref = bf16[32,4,128]{2,1,0:T(4,128)(2,1)S(1)} all-to-all(bf16[32,4,128]{2,1,0:T(4,128)(2,1)S(1)} %get-tuple-element.28), channel_id=1, replica_groups=mesh['gx'=4,'gy'=2,'gz'=4] {'gz','gx','gy'}, dimensions={0} | all-to-all | bytes 65536 | tf_op jit(solution)/shard_map/all_to_all | solution.py:332
  25.7 0.5 shard_map.70
  26.2 8.9 %all_to_all.27.received_ref = bf16[32,4,128]{2,1,0:T(4,128)(2,1)S(1)} all-to-all(bf16[32,4,128]{2,1,0:T(4,128)(2,1)S(1)} %get-tuple-element.35), channel_id=1, replica_groups=mesh['gx'=4,'gy'=2,'gz'=4] {'gz','gx','gy'}, dimensions={0} | all-to-all | bytes 65536 | tf_op jit(solution)/shard_map/all_to_all | solution.py:332
  35.1 0.5 shard_map.71
  35.6 8.9 %all_to_all.28.received_ref = bf16[32,4,128]{2,1,0:T(4,128)(2,1)S(1)} all-to-all(bf16[32,4,128]{2,1,0:T(4,128)(2,1)S(1)} %get-tuple-element.39), channel_id=1, replica_groups=mesh['gx'=4,'gy'=2,'gz'=4] {'gz','gx','gy'}, dimensions={0} | all-to-all | bytes 65536 | tf_op jit(solution)/shard_map/all_to_all | solution.py:332
  44.5 0.5 shard_map.72
  45.1 8.9 %all_to_all.29.received_ref = bf16[32,4,128]{2,1,0:T(4,128)(2,1)S(1)} all-to-all(bf16[32,4,128]{2,1,0:T(4,128)(2,1)S(1)} %get-tuple-element.43), channel_id=1, replica_groups=mesh['gx'=4,'gy'=2,'gz'=4] {'gz','gx','gy'}, dimensions={0} | all-to-all | bytes 65536 | tf_op jit(solution)/shard_map/all_to_all | solution.py:332
  53.9 1.1 %shard_map.73 = (f32[4,128]{1,0:T(4,128)}, f32[4,128]{1,0:T(4,128)}) custom-call(bf16[32,4,128]{2,1,0:T(4,128)(2,1)S(1)} %all_to_all.29.received_ref, bf16[2,1,2,27,128,128]{5,4,3,2,1,0:T(8,128)(2,1)S(1)} %copy-done, f32[3,18,128,128]{3,2,1,0:T(8,128)S(1)} %get-tuple-element.29.wide_ref, s32[192,128]{1,0:T(8,128)S(1)} %get-tuple-element.30.index_ref, ...), custom_call_target="tpu_custom_call" | custom-call | tf_op jit(solution)/shard_map/pallas_call | solution.py:379
Async XLA Ops:
  0.6 15.4 %copy-start = (bf16[2,1,2,27,128,128]{5,4,3,2,1,0:T(8,128)(2,1)S(1)}, bf16[2,1,2,27,128,128]{5,4,3,2,1,0:T(8,128)(2,1)}, u32[]{:S(2)}) copy-start(bf16[2,1,2,27,128,128]{5,4,3,2,1,0:T(8,128)(2,1)} %blocks_ref.9) | copy-start | bytes 10616836
  0.6 15.4 %copy-start.1 = (f32[2,1,2,128]{3,2,1,0:T(2,128)S(1)}, f32[2,1,2,128]{3,2,1,0:T(2,128)}, u32[]{:S(2)}) copy-start(f32[2,1,2,128]{3,2,1,0:T(2,128)} %param.8) | copy-start | bytes 6148
  0.7 15.4 %copy-start.2 = (f32[2,1,2,128]{3,2,1,0:T(2,128)S(1)}, f32[2,1,2,128]{3,2,1,0:T(2,128)}, u32[]{:S(2)}) copy-start(f32[2,1,2,128]{3,2,1,0:T(2,128)} %param.9) | copy-start | bytes 6148

commit v6 on v5

--- a/solution.py
+++ b/solution.py
@@ -198,7 +198,21 @@
     return blocks_ref[x, y, s, 9 * i + 3 * (j + plan.first_span()) + k]
 
 
-def product(plan, blocks_ref, wide_ref, received_ref, index_ref, mask_ref, gather_ref, opening=False):
+def tile_of(plan, block, row, group, tile_ref):
+    size = plan.width
+    for quad in group:
+        for part in range(4):
+            number = 4 * quad + part
+            line = size * (2 * quad + part % 2)
+            lane = size * (part // 2)
+            if number < len(plan.entries):
+                values = block(row, number).astype(jnp.float32).T.astype(jnp.bfloat16)
+            else:
+                values = jnp.zeros((size, size), jnp.bfloat16)
+            tile_ref[row, line : line + size, lane : lane + size] = values
+
+
+def product(plan, blocks_ref, tile_ref, wide_ref, received_ref, index_ref, mask_ref, gather_ref, opening=False):
     columns = gathered_columns(plan, received_ref, 0)
     for place, (row, i, j) in enumerate(plan.picks):
         here = slice(8 * place, 8 * place + 8)
@@ -227,25 +241,31 @@
         for group in (whole[:cut], whole[cut:], [plan.quads - 1] if plan.quads > len(whole) else []):
             if not group:
                 continue
+            if opening:
+                tile_of(plan, block, row, group, tile_ref)
             left, right = [], []
             for quad in group:
                 for side in (0, 1):
                     lines = [vectors(row, 4 * quad + side), vectors(row, 4 * quad + 2 + side)]
                     left.append(jnp.concatenate(lines, axis=0).astype(jnp.bfloat16))
-                parts = [pair(row, at) for at in (4 * quad, 4 * quad + 2) if at < count]
-                right.append(jnp.concatenate(parts, axis=0))
-            both = lax.dot_general(
-                jnp.concatenate(left, axis=1),
-                jnp.concatenate(right, axis=1),
-                (((1,), (1,)), ((), ())),
-                preferred_element_type=jnp.float32,
-            )
+                if opening:
+                    parts = [pair(row, at) for at in (4 * quad, 4 * quad + 2) if at < count]
+                    right.append(jnp.concatenate(parts, axis=0))
+            left = jnp.concatenate(left, axis=1)
+            if opening:
+                both = lax.dot_general(
+                    left,
+                    jnp.concatenate(right, axis=1),
+                    (((1,), (1,)), ((), ())),
+                    preferred_element_type=jnp.float32,
+                )
+            else:
+                here = slice(2 * size * group[0], 2 * size * (group[-1] + 1))
+                both = jnp.dot(left, tile_ref[row, here, :], preferred_element_type=jnp.float32)
             found = found + both[:1, :size]
             if both.shape[1] > size:
                 found = found + both[1:2, size:]
         results.append(found)
-    lane = lax.broadcasted_iota(jnp.int32, (size, size), 1)
-    line = lax.broadcasted_iota(jnp.int32, (size, size), 0)
     for place, row in enumerate(plan.plain):
         total = jnp.zeros((size, size), jnp.float32)
         for number in range(count):
@@ -255,20 +275,27 @@
             else:
                 values = wide_ref[place, number]
             total = total + values * vectors(row, number)
-        sums = jnp.sum(total, axis=1, keepdims=True)
-        results.append(jnp.sum(jnp.where(lane == line, sums, 0.0), axis=0, keepdims=True))
+        high = total.astype(jnp.bfloat16)
+        low = (total - high.astype(jnp.float32)).astype(jnp.bfloat16)
+        sums = lax.dot_general(
+            jnp.ones((8, 2 * size), jnp.bfloat16),
+            jnp.concatenate([high, low], axis=1),
+            (((1,), (1,)), ((), ())),
+            preferred_element_type=jnp.float32,
+        )
+        results.append(sums[:1])
     return jnp.concatenate(results, axis=0)
 
 
 def opening_kernel(
     plan, received_ref, blocks_ref, plane_ref, keep_ref, start_ref, rhs_ref,
-    pay_ref, index_ref, mask_ref, wide_ref, smoothed_ref, remainder_ref, search_ref,
+    pay_ref, index_ref, mask_ref, tile_ref, wide_ref, smoothed_ref, remainder_ref, search_ref,
     gather_ref, slots_ref, flags_ref,
 ):
     columns = gathered_columns(plan, received_ref, plan.rows)
     tables(plan, columns, plane_ref, keep_ref, slots_ref, flags_ref, index_ref, mask_ref)
     remainder = rhs_ref[...] - product(
-        plan, blocks_ref, wide_ref, received_ref, index_ref, mask_ref, gather_ref, True
+        plan, blocks_ref, tile_ref, wide_ref, received_ref, index_ref, mask_ref, gather_ref, True
     )
     search = remainder / CENTER
     send(search, pay_ref)
@@ -278,13 +305,13 @@
 
 
 def turn_kernel(
-    plan, factors, received_ref, blocks_ref, wide_ref, index_ref, mask_ref,
+    plan, factors, received_ref, tile_ref, wide_ref, index_ref, mask_ref,
     smoothed_in, remainder_in, search_in,
     pay_ref, smoothed_ref, remainder_ref, *rest,
 ):
     *search_ref, gather_ref = rest
     remainder = remainder_in[...] - product(
-        plan, blocks_ref, wide_ref, received_ref, index_ref, mask_ref, gather_ref
+        plan, None, tile_ref, wide_ref, received_ref, index_ref, mask_ref, gather_ref
     )
     search = factors[0] * search_in[...] + factors[1] * remainder
     send(search, pay_ref)
@@ -295,12 +322,12 @@
 
 
 def closing_kernel(
-    plan, received_ref, blocks_ref, wide_ref, index_ref, mask_ref, smoothed_in, remainder_in,
+    plan, received_ref, tile_ref, wide_ref, index_ref, mask_ref, smoothed_in, remainder_in,
     smoothed_ref, remainder_ref, gather_ref,
 ):
     smoothed_ref[...] = smoothed_in[...]
     remainder_ref[...] = remainder_in[...] - product(
-        plan, blocks_ref, wide_ref, received_ref, index_ref, mask_ref, gather_ref
+        plan, None, tile_ref, wide_ref, received_ref, index_ref, mask_ref, gather_ref
     )
 
 
@@ -345,13 +372,14 @@
         ],
         pl.CostEstimate(flops=10**10, bytes_accessed=10**8, transcendentals=0),
     )(far(order), far(pattern), far(flat_start))
-    sent, index, mask, wide, smoothed, remainder, *search = call(
+    sent, index, mask, tile, wide, smoothed, remainder, *search = call(
         functools.partial(opening_kernel, plan),
         [VMEM] * 6,
         [
             pay(plan.rows),
             like(jnp.int32, 8 * len(plan.picks), LANES),
             like(jnp.float32, 8 * len(plan.picks), LANES),
+            like(jnp.bfloat16, len(plan.tiled), 2 * width * plan.quads, 2 * width),
             like(jnp.float32, len(plan.plain), len(plan.entries), width, width),
             state,
             state,
@@ -375,10 +403,10 @@
             [VMEM] * 8,
             [pay(plan.rows)] + states,
             scratch,
-        )(exchange(sent), blocks, wide, index, mask, smoothed, remainder, *search)
+        )(exchange(sent), tile, wide, index, mask, smoothed, remainder, *search)
     smoothed, remainder = call(
         functools.partial(closing_kernel, plan), [VMEM] * 7, [state, state], scratch
-    )(exchange(sent), blocks, wide, index, mask, smoothed, remainder)
+    )(exchange(sent), tile, wide, index, mask, smoothed, remainder)
     return smoothed.reshape(start.shape), remainder.reshape(start.shape)
 
 

time: 55.3 us -> 55 us (level)
  no operation moved by 1% of the time
where the time goes in v6:
time: 55 us; the launch traced here: 54.8 us
  blocking collectives  49.9 us (91%)
  Pallas kernels  4.1 us (7%)
  between operations  0.7 us (1%)
    all_to_all x5, blocking collectives, exchange(): return lax.all_to_all(sent, AXES, 0, 0, tiled=True)  49.9 us
    pallas_call x3, Pallas kernels, local(): call(functools.partial(turn_kernel, plan, factors), [VMEM] * 8, [pay(plan...  1.39 us

profile of v6, /device:TPU:0, one launch (start us, length us, event | category | flops | bytes accessed | tf_op | source)
XLA Modules:
  0.0 54.8 jit_solution(4868281810886204933)
XLA Ops:
  0.6 0.0 copy-start
  0.6 0.0 copy-start.1
  0.7 0.0 copy-start.2
  0.7 1.0 %shard_map.68 = (bf16[32,8,128]{2,1,0:T(8,128)(2,1)S(1)}, f32[4,128]{1,0:T(4,128)S(1)}, f32[1,128]{1,0:T(1,128)S(1)}) custom-call(s32[2,1,8]{2,1,0:T(1,128)} %order_hbm.1, s32[2,1,8,27]{3,2,1,0:T(8,128)} %pattern_hbm.1, f32[4,128]{1,0:T(4,128)} %bitcast.8), custom_call_target="tpu_custom_call" | custom-call | flops 10000000000 | bytes 100000000 | tf_op jit(solution)/shard_map/pallas_call | solution.py:363
  1.6 14.4 %all_to_all.25.received_ref = bf16[32,8,128]{2,1,0:T(8,128)(2,1)S(1)} all-to-all(bf16[32,8,128]{2,1,0:T(8,128)(2,1)S(1)} %get-tuple-element.26), channel_id=1, replica_groups=mesh['gx'=4,'gy'=2,'gz'=4] {'gz','gx','gy'}, dimensions={0} | all-to-all | bytes 131072 | tf_op jit(solution)/shard_map/all_to_all | solution.py:359
  16.0 0.0 copy-done
  16.0 0.0 copy-done.1
  16.0 0.0 copy-done.2
  16.0 0.7 %shard_map.69 = (bf16[32,4,128]{2,1,0:T(4,128)(2,1)S(1)}, s32[192,128]{1,0:T(8,128)S(1)}, f32[192,128]{1,0:T(8,128)S(1)}, bf16[1,1280,256]{2,1,0:T(8,128)(2,1)S(...) custom-call(bf16[32,8,128]{2,1,0:T(8,128)(2,1)S(1)} %all_to_all.25.rec, ...), custom_call_target="tpu_custom_call" | custom-call | tf_op jit(solution)/shard_map/pallas_call | solution.py:375
  16.8 8.9 %all_to_all.26.received_ref = bf16[32,4,128]{2,1,0:T(4,128)(2,1)S(1)} all-to-all(bf16[32,4,128]{2,1,0:T(4,128)(2,1)S(1)} %get-tuple-element.29), channel_id=1, replica_groups=mesh['gx'=4,'gy'=2,'gz'=4] {'gz','gx','gy'}, dimensions={0} | all-to-all | bytes 65536 | tf_op jit(solution)/shard_map/all_to_all | solution.py:359
  25.7 0.5 shard_map.70
  26.1 8.9 %all_to_all.27.received_ref = bf16[32,4,128]{2,1,0:T(4,128)(2,1)S(1)} all-to-all(bf16[32,4,128]{2,1,0:T(4,128)(2,1)S(1)} %get-tuple-element.37), channel_id=1, replica_groups=mesh['gx'=4,'gy'=2,'gz'=4] {'gz','gx','gy'}, dimensions={0} | all-to-all | bytes 65536 | tf_op jit(solution)/shard_map/all_to_all | solution.py:359
  35.0 0.5 shard_map.71
  35.5 8.9 %all_to_all.28.received_ref = bf16[32,4,128]{2,1,0:T(4,128)(2,1)S(1)} all-to-all(bf16[32,4,128]{2,1,0:T(4,128)(2,1)S(1)} %get-tuple-element.41), channel_id=1, replica_groups=mesh['gx'=4,'gy'=2,'gz'=4] {'gz','gx','gy'}, dimensions={0} | all-to-all | bytes 65536 | tf_op jit(solution)/shard_map/all_to_all | solution.py:359
  44.4 0.5 shard_map.72
  44.8 8.9 %all_to_all.29.received_ref = bf16[32,4,128]{2,1,0:T(4,128)(2,1)S(1)} all-to-all(bf16[32,4,128]{2,1,0:T(4,128)(2,1)S(1)} %get-tuple-element.45), channel_id=1, replica_groups=mesh['gx'=4,'gy'=2,'gz'=4] {'gz','gx','gy'}, dimensions={0} | all-to-all | bytes 65536 | tf_op jit(solution)/shard_map/all_to_all | solution.py:359
  53.7 1.0 %shard_map.73 = (f32[4,128]{1,0:T(4,128)}, f32[4,128]{1,0:T(4,128)}) custom-call(bf16[32,4,128]{2,1,0:T(4,128)(2,1)S(1)} %all_to_all.29.received_ref, bf16[1,1280,256]{2,1,0:T(8,128)(2,1)S(1)} %get-tuple-element.30.tile_ref, f32[3,18,128,128]{3,2,1,0:T(8,128)S(1)} %get-tuple-element.31.wide_ref, s32[192,128]{1,0:T(8,128)S(1)} %get-tuple-element.32.index_ref, ...), custom_call_target="tpu_custom_call" | custom-call | tf_op jit(solution)/shard_map/pallas_call | solution.py:407
Async XLA Ops:
  0.6 15.4 %copy-start = (bf16[2,1,2,27,128,128]{5,4,3,2,1,0:T(8,128)(2,1)S(1)}, bf16[2,1,2,27,128,128]{5,4,3,2,1,0:T(8,128)(2,1)}, u32[]{:S(2)}) copy-start(bf16[2,1,2,27,128,128]{5,4,3,2,1,0:T(8,128)(2,1)} %blocks_ref.1) | copy-start | bytes 10616836
  0.6 15.4 %copy-start.1 = (f32[2,1,2,128]{3,2,1,0:T(2,128)S(1)}, f32[2,1,2,128]{3,2,1,0:T(2,128)}, u32[]{:S(2)}) copy-start(f32[2,1,2,128]{3,2,1,0:T(2,128)} %param.8) | copy-start | bytes 6148
  0.7 15.4 %copy-start.2 = (f32[2,1,2,128]{3,2,1,0:T(2,128)S(1)}, f32[2,1,2,128]{3,2,1,0:T(2,128)}, u32[]{:S(2)}) copy-start(f32[2,1,2,128]{3,2,1,0:T(2,128)} %param.9) | copy-start | bytes 6148

commit v7 on v6

--- a/solution.py
+++ b/solution.py
@@ -210,6 +210,24 @@
             else:
                 values = jnp.zeros((size, size), jnp.bfloat16)
             tile_ref[row, line : line + size, lane : lane + size] = values
+
+
+def lane_sums(total, multiplied):
+    size = total.shape[0]
+    if multiplied:
+        high = total.astype(jnp.bfloat16)
+        low = (total - high.astype(jnp.float32)).astype(jnp.bfloat16)
+        sums = lax.dot_general(
+            jnp.ones((8, 2 * size), jnp.bfloat16),
+            jnp.concatenate([high, low], axis=1),
+            (((1,), (1,)), ((), ())),
+            preferred_element_type=jnp.float32,
+        )
+        return sums[:1]
+    lane = lax.broadcasted_iota(jnp.int32, (size, size), 1)
+    line = lax.broadcasted_iota(jnp.int32, (size, size), 0)
+    sums = jnp.sum(total, axis=1, keepdims=True)
+    return jnp.sum(jnp.where(lane == line, sums, 0.0), axis=0, keepdims=True)
 
 
 def product(plan, blocks_ref, tile_ref, wide_ref, received_ref, index_ref, mask_ref, gather_ref, opening=False):
@@ -275,15 +293,7 @@
             else:
                 values = wide_ref[place, number]
             total = total + values * vectors(row, number)
-        high = total.astype(jnp.bfloat16)
-        low = (total - high.astype(jnp.float32)).astype(jnp.bfloat16)
-        sums = lax.dot_general(
-            jnp.ones((8, 2 * size), jnp.bfloat16),
-            jnp.concatenate([high, low], axis=1),
-            (((1,), (1,)), ((), ())),
-            preferred_element_type=jnp.float32,
-        )
-        results.append(sums[:1])
+        results.append(lane_sums(total, opening or row != plan.plain[-1]))
     return jnp.concatenate(results, axis=0)
 
 

time: 55 us -> 54.9 us (level)
  no operation moved by 1% of the time
where the time goes in v7:
time: 54.9 us; the launch traced here: 54.6 us
  blocking collectives  49.9 us (91%)
  Pallas kernels  3.94 us (7%)
  between operations  0.69 us (1%)
    all_to_all x5, blocking collectives, exchange(): return lax.all_to_all(sent, AXES, 0, 0, tiled=True)  49.9 us
    pallas_call x3, Pallas kernels, local(): call(functools.partial(turn_kernel, plan, factors), [VMEM] * 8, [pay(plan...  1.28 us

profile of v7, /device:TPU:0, one launch (start us, length us, event | category | flops | bytes accessed | tf_op | source)
XLA Modules:
  0.0 54.6 jit_solution(10727852373420856334)
XLA Ops:
  0.6 0.0 copy-start
  0.6 0.0 copy-start.1
  0.7 0.0 copy-start.2
  0.7 1.0 %shard_map.68 = (bf16[32,8,128]{2,1,0:T(8,128)(2,1)S(1)}, f32[4,128]{1,0:T(4,128)S(1)}, f32[1,128]{1,0:T(1,128)S(1)}) custom-call(s32[2,1,8]{2,1,0:T(1,128)} %order_hbm.1, s32[2,1,8,27]{3,2,1,0:T(8,128)} %pattern_hbm.1, f32[4,128]{1,0:T(4,128)} %bitcast.8), custom_call_target="tpu_custom_call" | custom-call | flops 10000000000 | bytes 100000000 | tf_op jit(solution)/shard_map/pallas_call | solution.py:373
  1.6 14.4 %all_to_all.25.received_ref = bf16[32,8,128]{2,1,0:T(8,128)(2,1)S(1)} all-to-all(bf16[32,8,128]{2,1,0:T(8,128)(2,1)S(1)} %get-tuple-element.26), channel_id=1, replica_groups=mesh['gx'=4,'gy'=2,'gz'=4] {'gz','gx','gy'}, dimensions={0} | all-to-all | bytes 131072 | tf_op jit(solution)/shard_map/all_to_all | solution.py:369
  16.0 0.0 copy-done
  16.0 0.0 copy-done.1
  16.0 0.0 copy-done.2
  16.0 0.7 %shard_map.69 = (bf16[32,4,128]{2,1,0:T(4,128)(2,1)S(1)}, s32[192,128]{1,0:T(8,128)S(1)}, f32[192,128]{1,0:T(8,128)S(1)}, bf16[1,1280,256]{2,1,0:T(8,128)(2,1)S(...) custom-call(bf16[32,8,128]{2,1,0:T(8,128)(2,1)S(1)} %all_to_all.25.rec, ...), custom_call_target="tpu_custom_call" | custom-call | tf_op jit(solution)/shard_map/pallas_call | solution.py:385
  16.8 8.9 %all_to_all.26.received_ref = bf16[32,4,128]{2,1,0:T(4,128)(2,1)S(1)} all-to-all(bf16[32,4,128]{2,1,0:T(4,128)(2,1)S(1)} %get-tuple-element.29), channel_id=1, replica_groups=mesh['gx'=4,'gy'=2,'gz'=4] {'gz','gx','gy'}, dimensions={0} | all-to-all | bytes 65536 | tf_op jit(solution)/shard_map/all_to_all | solution.py:369
  25.7 0.4 shard_map.70
  26.1 8.9 %all_to_all.27.received_ref = bf16[32,4,128]{2,1,0:T(4,128)(2,1)S(1)} all-to-all(bf16[32,4,128]{2,1,0:T(4,128)(2,1)S(1)} %get-tuple-element.37), channel_id=1, replica_groups=mesh['gx'=4,'gy'=2,'gz'=4] {'gz','gx','gy'}, dimensions={0} | all-to-all | bytes 65536 | tf_op jit(solution)/shard_map/all_to_all | solution.py:369
  35.0 0.4 shard_map.71
  35.4 8.9 %all_to_all.28.received_ref = bf16[32,4,128]{2,1,0:T(4,128)(2,1)S(1)} all-to-all(bf16[32,4,128]{2,1,0:T(4,128)(2,1)S(1)} %get-tuple-element.41), channel_id=1, replica_groups=mesh['gx'=4,'gy'=2,'gz'=4] {'gz','gx','gy'}, dimensions={0} | all-to-all | bytes 65536 | tf_op jit(solution)/shard_map/all_to_all | solution.py:369
  44.3 0.4 shard_map.72
  44.7 8.9 %all_to_all.29.received_ref = bf16[32,4,128]{2,1,0:T(4,128)(2,1)S(1)} all-to-all(bf16[32,4,128]{2,1,0:T(4,128)(2,1)S(1)} %get-tuple-element.45), channel_id=1, replica_groups=mesh['gx'=4,'gy'=2,'gz'=4] {'gz','gx','gy'}, dimensions={0} | all-to-all | bytes 65536 | tf_op jit(solution)/shard_map/all_to_all | solution.py:369
  53.6 1.0 %shard_map.73 = (f32[4,128]{1,0:T(4,128)}, f32[4,128]{1,0:T(4,128)}) custom-call(bf16[32,4,128]{2,1,0:T(4,128)(2,1)S(1)} %all_to_all.29.received_ref, bf16[1,1280,256]{2,1,0:T(8,128)(2,1)S(1)} %get-tuple-element.30.tile_ref, f32[3,18,128,128]{3,2,1,0:T(8,128)S(1)} %get-tuple-element.31.wide_ref, s32[192,128]{1,0:T(8,128)S(1)} %get-tuple-element.32.index_ref, ...), custom_call_target="tpu_custom_call" | custom-call | tf_op jit(solution)/shard_map/pallas_call | solution.py:417
Async XLA Ops:
  0.6 15.4 %copy-start = (bf16[2,1,2,27,128,128]{5,4,3,2,1,0:T(8,128)(2,1)S(1)}, bf16[2,1,2,27,128,128]{5,4,3,2,1,0:T(8,128)(2,1)}, u32[]{:S(2)}) copy-start(bf16[2,1,2,27,128,128]{5,4,3,2,1,0:T(8,128)(2,1)} %blocks_ref.1) | copy-start | bytes 10616836
  0.6 15.4 %copy-start.1 = (f32[2,1,2,128]{3,2,1,0:T(2,128)S(1)}, f32[2,1,2,128]{3,2,1,0:T(2,128)}, u32[]{:S(2)}) copy-start(f32[2,1,2,128]{3,2,1,0:T(2,128)} %param.8) | copy-start | bytes 6148
  0.7 15.4 %copy-start.2 = (f32[2,1,2,128]{3,2,1,0:T(2,128)S(1)}, f32[2,1,2,128]{3,2,1,0:T(2,128)}, u32[]{:S(2)}) copy-start(f32[2,1,2,128]{3,2,1,0:T(2,128)} %param.9) | copy-start | bytes 6148

commit v8 on v7

--- a/solution.py
+++ b/solution.py
@@ -80,10 +80,12 @@
         pltpu.make_async_copy(pattern_hbm, pattern_ref, sems.at[1]),
         pltpu.make_async_copy(start_hbm, start_ref, sems.at[2]),
     )
-    for copy in copies:
+    for copy in (copies[1], copies[0], copies[2]):
         copy.start()
-    for copy in copies:
-        copy.wait()
+    copies[1].wait()
+    keep_ref[...] = kept(plan, pattern_ref)
+    copies[0].wait()
+    copies[2].wait()
     first = lax.axis_index("gz") * plan.nz
     line = lax.broadcasted_iota(jnp.int32, (plan.rows, plan.width), 0)
     planes = jnp.zeros_like(line)
@@ -93,7 +95,6 @@
     planes = planes.astype(jnp.float32)
     send(jnp.concatenate([start_ref[...], planes], axis=0), pay_ref)
     plane_ref[...] = planes
-    keep_ref[...] = kept(plan, pattern_ref)
 
 
 def kept(plan, pattern_ref):
@@ -259,8 +260,6 @@
         for group in (whole[:cut], whole[cut:], [plan.quads - 1] if plan.quads > len(whole) else []):
             if not group:
                 continue
-            if opening:
-                tile_of(plan, block, row, group, tile_ref)
             left, right = [], []
             for quad in group:
                 for side in (0, 1):
@@ -294,6 +293,9 @@
                 values = wide_ref[place, number]
             total = total + values * vectors(row, number)
         results.append(lane_sums(total, opening or row != plan.plain[-1]))
+    if opening:
+        for row in plan.tiled:
+            tile_of(plan, block, row, range(plan.quads), tile_ref)
     return jnp.concatenate(results, axis=0)
 
 

time: 54.9 us -> 54.9 us (level)
  no operation moved by 1% of the time
where the time goes in v8:
time: 54.9 us; the launch traced here: 54.6 us
  blocking collectives  49.9 us (91%)
  Pallas kernels  3.97 us (7%)
  between operations  0.69 us (1%)
    all_to_all x5, blocking collectives, exchange(): return lax.all_to_all(sent, AXES, 0, 0, tiled=True)  49.9 us
    pallas_call x3, Pallas kernels, local(): call(functools.partial(turn_kernel, plan, factors), [VMEM] * 8, [pay(plan...  1.28 us

profile of v8, /device:TPU:0, one launch (start us, length us, event | category | flops | bytes accessed | tf_op | source)
XLA Modules:
  0.0 54.6 jit_solution(14326255316837324818)
XLA Ops:
  0.6 0.0 copy-start
  0.6 0.0 copy-start.1
  0.7 0.0 copy-start.2
  0.7 1.0 %shard_map.68 = (bf16[32,8,128]{2,1,0:T(8,128)(2,1)S(1)}, f32[4,128]{1,0:T(4,128)S(1)}, f32[1,128]{1,0:T(1,128)S(1)}) custom-call(s32[2,1,8]{2,1,0:T(1,128)} %order_hbm.1, s32[2,1,8,27]{3,2,1,0:T(8,128)} %pattern_hbm.1, f32[4,128]{1,0:T(4,128)} %bitcast.8), custom_call_target="tpu_custom_call" | custom-call | flops 10000000000 | bytes 100000000 | tf_op jit(solution)/shard_map/pallas_call | solution.py:375
  1.6 14.4 %all_to_all.25.received_ref = bf16[32,8,128]{2,1,0:T(8,128)(2,1)S(1)} all-to-all(bf16[32,8,128]{2,1,0:T(8,128)(2,1)S(1)} %get-tuple-element.26), channel_id=1, replica_groups=mesh['gx'=4,'gy'=2,'gz'=4] {'gz','gx','gy'}, dimensions={0} | all-to-all | bytes 131072 | tf_op jit(solution)/shard_map/all_to_all | solution.py:371
  16.1 0.0 copy-done
  16.1 0.0 copy-done.1
  16.1 0.0 copy-done.2
  16.1 0.7 %shard_map.69 = (bf16[32,4,128]{2,1,0:T(4,128)(2,1)S(1)}, s32[192,128]{1,0:T(8,128)S(1)}, f32[192,128]{1,0:T(8,128)S(1)}, bf16[1,1280,256]{2,1,0:T(8,128)(2,1)S(...) custom-call(bf16[32,8,128]{2,1,0:T(8,128)(2,1)S(1)} %all_to_all.25.rec, ...), custom_call_target="tpu_custom_call" | custom-call | tf_op jit(solution)/shard_map/pallas_call | solution.py:387
  16.8 8.9 %all_to_all.26.received_ref = bf16[32,4,128]{2,1,0:T(4,128)(2,1)S(1)} all-to-all(bf16[32,4,128]{2,1,0:T(4,128)(2,1)S(1)} %get-tuple-element.29), channel_id=1, replica_groups=mesh['gx'=4,'gy'=2,'gz'=4] {'gz','gx','gy'}, dimensions={0} | all-to-all | bytes 65536 | tf_op jit(solution)/shard_map/all_to_all | solution.py:371
  25.7 0.4 shard_map.70
  26.1 8.9 %all_to_all.27.received_ref = bf16[32,4,128]{2,1,0:T(4,128)(2,1)S(1)} all-to-all(bf16[32,4,128]{2,1,0:T(4,128)(2,1)S(1)} %get-tuple-element.37), channel_id=1, replica_groups=mesh['gx'=4,'gy'=2,'gz'=4] {'gz','gx','gy'}, dimensions={0} | all-to-all | bytes 65536 | tf_op jit(solution)/shard_map/all_to_all | solution.py:371
  35.0 0.4 shard_map.71
  35.4 8.9 %all_to_all.28.received_ref = bf16[32,4,128]{2,1,0:T(4,128)(2,1)S(1)} all-to-all(bf16[32,4,128]{2,1,0:T(4,128)(2,1)S(1)} %get-tuple-element.41), channel_id=1, replica_groups=mesh['gx'=4,'gy'=2,'gz'=4] {'gz','gx','gy'}, dimensions={0} | all-to-all | bytes 65536 | tf_op jit(solution)/shard_map/all_to_all | solution.py:371
  44.3 0.4 shard_map.72
  44.7 8.9 %all_to_all.29.received_ref = bf16[32,4,128]{2,1,0:T(4,128)(2,1)S(1)} all-to-all(bf16[32,4,128]{2,1,0:T(4,128)(2,1)S(1)} %get-tuple-element.45), channel_id=1, replica_groups=mesh['gx'=4,'gy'=2,'gz'=4] {'gz','gx','gy'}, dimensions={0} | all-to-all | bytes 65536 | tf_op jit(solution)/shard_map/all_to_all | solution.py:371
  53.6 1.0 %shard_map.73 = (f32[4,128]{1,0:T(4,128)}, f32[4,128]{1,0:T(4,128)}) custom-call(bf16[32,4,128]{2,1,0:T(4,128)(2,1)S(1)} %all_to_all.29.received_ref, bf16[1,1280,256]{2,1,0:T(8,128)(2,1)S(1)} %get-tuple-element.30.tile_ref, f32[3,18,128,128]{3,2,1,0:T(8,128)S(1)} %get-tuple-element.31.wide_ref, s32[192,128]{1,0:T(8,128)S(1)} %get-tuple-element.32.index_ref, ...), custom_call_target="tpu_custom_call" | custom-call | tf_op jit(solution)/shard_map/pallas_call | solution.py:419
Async XLA Ops:
  0.6 15.4 %copy-start = (bf16[2,1,2,27,128,128]{5,4,3,2,1,0:T(8,128)(2,1)S(1)}, bf16[2,1,2,27,128,128]{5,4,3,2,1,0:T(8,128)(2,1)}, u32[]{:S(2)}) copy-start(bf16[2,1,2,27,128,128]{5,4,3,2,1,0:T(8,128)(2,1)} %blocks_ref.1) | copy-start | bytes 10616836
  0.6 15.4 %copy-start.1 = (f32[2,1,2,128]{3,2,1,0:T(2,128)S(1)}, f32[2,1,2,128]{3,2,1,0:T(2,128)}, u32[]{:S(2)}) copy-start(f32[2,1,2,128]{3,2,1,0:T(2,128)} %param.8) | copy-start | bytes 6148
  0.7 15.4 %copy-start.2 = (f32[2,1,2,128]{3,2,1,0:T(2,128)S(1)}, f32[2,1,2,128]{3,2,1,0:T(2,128)}, u32[]{:S(2)}) copy-start(f32[2,1,2,128]{3,2,1,0:T(2,128)} %param.9) | copy-start | bytes 6148
